TPU v7x, 32 devices: a whole 2x2x4 slice. The times are simulated.
32 devices in a mesh: inst: 2 (over x), qy: 4 (over z), qx: 4 (over y, core).
Axes of the slice: x: 2, y: 2, z: 4, core: 2. Of those that a mesh axis runs over, the one named last changes fastest.
Arguments:
- cost: float32 [2097152], P(('inst', 'qy', 'qx')), parts along dimension 0
- gamma: float32 [4, 5], P('inst'), parts along dimension 0
- beta: float32 [4, 5], P('inst'), parts along dimension 0
Outputs:
- output 1: float32 [4], P('inst'), parts along dimension 0
- output 2: float32 [4, 10], P('inst'), parts along dimension 0
There are 2 independent parts. A program takes and returns all parts, laid end to end along the dimension named above; each array names one.
All inputs are finite; a program needn't handle non-finite values.
Results may differ from a plain program's by a relative error of at most 0.001.
Values sent between devices are 32-bit elements.
A program may use at most 1 GiB of HBM per device.

v0:
```python
import jax
import jax.numpy as jnp
from jax import lax
from jax.sharding import PartitionSpec as P

LANE_BITS = 7
LANE_WIDTH = 128


def flip_grid(amplitudes, qubit):
    if qubit < LANE_BITS:
        shift = 2 ** qubit
        position = lax.broadcasted_iota(jnp.int32, (LANE_WIDTH,), 0)
        axis_pos = amplitudes.ndim - 1
    else:
        shift = 2 ** (qubit - LANE_BITS)
        position = lax.broadcasted_iota(jnp.int32, (amplitudes.shape[-2], 1), 0)
        axis_pos = amplitudes.ndim - 2
    upper = (position & shift) != 0
    return jnp.where(upper, jnp.roll(amplitudes, shift, axis=axis_pos), jnp.roll(amplitudes, -shift, axis=axis_pos))


def partner_tables(mesh):
    tables = []
    for axis_name in ('qx', 'qy'):
        width = mesh.shape[axis_name]
        for bit_pos in range(width.bit_length() - 1):
            tables.append((axis_name, [(index, index ^ (1 << bit_pos)) for index in range(width)]))
    return tables


def inverse_step(four_amps, partner, cos_b, sin_b):
    psi_re, psi_im, lam_re, lam_im = four_amps
    term = jnp.sum(lam_re * partner[1] - lam_im * partner[0], axis=(1, 2))
    updated = (cos_b * psi_re - sin_b * partner[1], cos_b * psi_im + sin_b * partner[0], cos_b * lam_re - sin_b * partner[3], cos_b * lam_im + sin_b * partner[2])
    return updated, term


def solution(mesh):
    partners = partner_tables(mesh)
    global_count = len(partners)
    group_axes = ('qy', 'qx')

    def device_fn(cost, gamma, beta):
        local_size = cost.shape[0]
        local_count = local_size.bit_length() - 1
        row_count = local_size // LANE_WIDTH
        num_sets, num_layers = gamma.shape
        start_amp = 2.0 ** (-0.5 * (local_count + global_count))
        cost_grid = cost.reshape(1, row_count, LANE_WIDTH)
        gamma_grid = gamma[:, :, None, None]
        half_cos = jnp.cos(0.5 * beta)[:, :, None, None]
        half_sin = jnp.sin(0.5 * beta)[:, :, None, None]
        psi_re = jnp.full((num_sets, row_count, LANE_WIDTH), start_amp, jnp.float32)
        psi_im = jnp.zeros_like(psi_re)
        phase_saved = []
        for layer in range(num_layers):
            phase = gamma_grid[:, layer] * cost_grid
            cos_p = jnp.cos(phase)
            sin_p = jnp.sin(phase)
            phase_saved.append((cos_p, sin_p))
            psi_re, psi_im = psi_re * cos_p + psi_im * sin_p, psi_im * cos_p - psi_re * sin_p
            cos_b = half_cos[:, layer]
            sin_b = half_sin[:, layer]
            for qubit in range(local_count):
                flip_re = flip_grid(psi_re, qubit)
                flip_im = flip_grid(psi_im, qubit)
                psi_re, psi_im = cos_b * psi_re + sin_b * flip_im, cos_b * psi_im - sin_b * flip_re
            for axis_name, pair_list in partners:
                partner = lax.ppermute(jnp.stack([psi_re, psi_im]), axis_name, pair_list)
                psi_re, psi_im = cos_b * psi_re + sin_b * partner[1], cos_b * psi_im - sin_b * partner[0]
        energy_part = jnp.sum(cost_grid * (psi_re * psi_re + psi_im * psi_im), axis=(1, 2))
        four_amps = (psi_re, psi_im, cost_grid * psi_re, cost_grid * psi_im)
        gamma_grads = [None] * num_layers
        beta_grads = [None] * num_layers
        for layer in reversed(range(num_layers)):
            cos_b = half_cos[:, layer]
            sin_b = half_sin[:, layer]
            beta_term = jnp.zeros((num_sets,), jnp.float32)
            for qubit in range(local_count):
                flips = [flip_grid(amplitudes, qubit) for amplitudes in four_amps]
                four_amps, term = inverse_step(four_amps, flips, cos_b, sin_b)
                beta_term = beta_term + term
            for axis_name, pair_list in partners:
                partner = lax.ppermute(jnp.stack(list(four_amps)), axis_name, pair_list)
                four_amps, term = inverse_step(four_amps, partner, cos_b, sin_b)
                beta_term = beta_term + term
            psi_re, psi_im, lam_re, lam_im = four_amps
            beta_grads[layer] = beta_term
            gamma_grads[layer] = 2.0 * jnp.sum(cost_grid * (lam_re * psi_im - lam_im * psi_re), axis=(1, 2))
            if layer > 0:
                cos_p, sin_p = phase_saved[layer]
                four_amps = (psi_re * cos_p - psi_im * sin_p, psi_im * cos_p + psi_re * sin_p, lam_re * cos_p - lam_im * sin_p, lam_im * cos_p + lam_re * sin_p)
        grad_rows = jnp.stack(gamma_grads + beta_grads, axis=1)
        totals = lax.psum(jnp.concatenate([energy_part[:, None], grad_rows], axis=1), group_axes)
        return totals[:, 0], totals[:, 1:]

    cost_spec = P(('inst', 'qy', 'qx'))
    angle_spec = P('inst', None)
    return jax.shard_map(device_fn, mesh=mesh, in_specs=(cost_spec, angle_spec, angle_spec), out_specs=(P('inst'), angle_spec), check_vma=False)
```

profile of v0, /device:TPU:0, one launch (start us, length us, event | category | flops | bytes accessed | tf_op | source)
XLA Modules:
  0.0 2429.9 jit_solution(14046525904456914180)
XLA Ops:
  2.4 8.9 fusion.57
  16.3 9.2 fusion.58
  33.5 11.9 fusion.213
  120.7 5.8 fusion.249
  130.7 5.6 fusion.251
  159.5 7.9 fusion.265
  177.8 44.1 %fusion.338 = f32[1,2,512,128]{3,1,2,0:T(2,128)S(1)} fusion(f32[1,2,384,128]{3,1,2,0:T(2,128)} %get-tuple-element.2895, f32[1,2,128,128]{3,1,2,0:T(2,128)} %get-tuple-element.2899, f32[1,2,128,128]{3,1,2,0:T(2,128)} %get-tuple-element.2900, f32[1,2,384,128]{3,1,2,0:T(2,128)} %get-tuple-element.2896, f32[1,2,256,128]{3,1,2,0:T(2,128)S(1)} %get-tuple-element.2672, ...), kind=kLoop, calls=%fused_computation.552 | loop fusion | flops 12582912 | bytes 16519960 | tf_op jit(solution)/shard_map/sub | solution.py:68
  222.2 40.0 %fusion.303 = f32[1,2,512,128]{3,1,2,0:T(2,128)S(1)} fusion(f32[1,2,384,128]{3,1,2,0:T(2,128)} %get-tuple-element.2783, f32[1,2,128,128]{3,1,2,0:T(2,128)} %get-tuple-element.2787, f32[1,2,128,128]{3,1,2,0:T(2,128)} %get-tuple-element.2786, f32[1,2,384,128]{3,1,2,0:T(2,128)} %get-tuple-element.2782, f32[1,2,256,128]{3,1,2,0:T(2,128)S(1)} %get-tuple-element.2676, ...), kind=kLoop, calls=%fused_computation.501 | loop fusion | flops 12582912 | bytes 16519960 | tf_op jit(solution)/shard_map/add | solution.py:68
  269.5 23.5 collective-permute-done.1
  295.9 22.8 collective-permute-done.2
  326.9 40.1 %collective-permute-done.3 = f32[2,2,512,128]{3,1,2,0:T(2,128)S(1)} collective-permute-done((f32[2,2,512,128]{3,1,2,0:T(2,128)S(1)}, f32[2,2,512,128]{3,1,2,0:T(2,128)S(1)}, u32[]{:S(2)}, u32[]{:S(2)}) %collective-permute-start.3) | collective-permute-done | bytes 1048608 | tf_op jit(solution)/shard_map/ppermute | solution.py:70
  483.6 7.0 fusion.391
  494.9 8.2 fusion.392
  521.2 9.8 fusion.435
  531.2 8.6 fusion.436
  540.1 28.5 %fusion.1059 = (f32[1,2,512,128]{3,1,2,0:T(2,128)S(1)}, f32[1,2,512,128]{3,1,2,0:T(2,128)S(1)}) fusion(f32[1,2,8,128]{3,1,2,0:T(2,128)} %get-tuple-element.2539, f32[1,2,504,128]{3,1,2,0:T(2,128)} %get-tuple-element.2543, f32[1,2,504,128]{3,1,2,0:T(2,128)} %get-tuple-element.2542, f32[1,2,8,128]{3,1,2,0:T(2,128)S(1)} %get-tuple-element.2538, ...), kind=kLoop, calls=%fused_computation.2187 | loop fusion | flops 9437184 | bytes 13896488 | tf_op jit(solution)/shard_map/mul | solution.py:68
  570.5 15.4 broadcast_multiply_fusion.3
  602.5 24.0 collective-permute-done.5
  627.5 24.1 collective-permute-done.6
  655.2 44.9 %collective-permute-done.7 = f32[2,2,512,128]{3,1,2,0:T(2,128)S(1)} collective-permute-done((f32[2,2,512,128]{3,1,2,0:T(2,128)S(1)}, f32[2,2,512,128]{3,1,2,0:T(2,128)S(1)}, u32[]{:S(2)}, u32[]{:S(2)}) %collective-permute-start.7) | collective-permute-done | bytes 1048608 | tf_op jit(solution)/shard_map/ppermute | solution.py:70
  818.3 6.3 fusion.520
  835.0 6.5 fusion.579
  841.6 7.5 copy_multiply_fusion.1
  859.4 24.0 collective-permute-done.9
  884.0 24.1 collective-permute-done.10
  910.3 44.9 %collective-permute-done.11 = f32[2,2,512,128]{3,2,1,0:T(8,128)S(1)} collective-permute-done((f32[2,2,512,128]{3,2,1,0:T(8,128)S(1)}, f32[2,2,512,128]{3,2,1,0:T(8,128)S(1)}, u32[]{:S(2)}, u32[]{:S(2)}) %collective-permute-start.11) | collective-permute-done | bytes 1048608 | tf_op jit(solution)/shard_map/ppermute | solution.py:70
  978.5 24.0 collective-permute-done.13
  1003.3 24.1 collective-permute-done.14
  1029.8 44.9 %collective-permute-done.15 = f32[2,2,512,128]{3,2,1,0:T(8,128)S(1)} collective-permute-done((f32[2,2,512,128]{3,2,1,0:T(8,128)S(1)}, f32[2,2,512,128]{3,2,1,0:T(8,128)S(1)}, u32[]{:S(2)}, u32[]{:S(2)}) %collective-permute-start.15) | collective-permute-done | bytes 1048608 | tf_op jit(solution)/shard_map/ppermute | solution.py:70
  1096.9 24.0 collective-permute-done.17
  1121.6 24.2 collective-permute-done.18
  1148.4 45.0 %collective-permute-done.19 = f32[2,2,512,128]{3,2,1,0:T(8,128)S(1)} collective-permute-done((f32[2,2,512,128]{3,2,1,0:T(8,128)S(1)}, f32[2,2,512,128]{3,2,1,0:T(8,128)S(1)}, u32[]{:S(2)}, u32[]{:S(2)}) %collective-permute-start.19) | collective-permute-done | bytes 1048608 | tf_op jit(solution)/shard_map/ppermute | solution.py:70
  1241.0 46.5 %collective-permute-done.21 = f32[4,2,512,128]{3,2,1,0:T(8,128)S(1)} collective-permute-done((f32[4,2,512,128]{3,2,1,0:T(8,128)S(1)}, f32[4,2,512,128]{3,2,1,0:T(8,128)S(1)}, u32[]{:S(2)}, u32[]{:S(2)}) %collective-permute-start.21) | collective-permute-done | bytes 2097184 | tf_op jit(solution)/shard_map/ppermute | solution.py:85
  1288.9 46.7 %collective-permute-done.22 = f32[4,2,512,128]{3,2,1,0:T(8,128)S(1)} collective-permute-done((f32[4,2,512,128]{3,2,1,0:T(8,128)S(1)}, f32[4,2,512,128]{3,2,1,0:T(8,128)S(1)}, u32[]{:S(2)}, u32[]{:S(2)}) %collective-permute-start.22) | collective-permute-done | bytes 2097184 | tf_op jit(solution)/shard_map/ppermute | solution.py:85
  1338.6 89.9 %collective-permute-done.23 = f32[4,2,512,128]{3,2,1,0:T(8,128)S(1)} collective-permute-done((f32[4,2,512,128]{3,2,1,0:T(8,128)S(1)}, f32[4,2,512,128]{3,2,1,0:T(8,128)S(1)}, u32[]{:S(2)}, u32[]{:S(2)}) %collective-permute-start.23) | collective-permute-done | bytes 2097184 | tf_op jit(solution)/shard_map/ppermute | solution.py:85
  1483.4 46.5 %collective-permute-done.25 = f32[4,2,512,128]{3,2,1,0:T(8,128)S(1)} collective-permute-done((f32[4,2,512,128]{3,2,1,0:T(8,128)S(1)}, f32[4,2,512,128]{3,2,1,0:T(8,128)S(1)}, u32[]{:S(2)}, u32[]{:S(2)}) %collective-permute-start.25) | collective-permute-done | bytes 2097184 | tf_op jit(solution)/shard_map/ppermute | solution.py:85
  1531.4 46.7 %collective-permute-done.26 = f32[4,2,512,128]{3,2,1,0:T(8,128)S(1)} collective-permute-done((f32[4,2,512,128]{3,2,1,0:T(8,128)S(1)}, f32[4,2,512,128]{3,2,1,0:T(8,128)S(1)}, u32[]{:S(2)}, u32[]{:S(2)}) %collective-permute-start.26) | collective-permute-done | bytes 2097184 | tf_op jit(solution)/shard_map/ppermute | solution.py:85
  1581.0 89.9 %collective-permute-done.27 = f32[4,2,512,128]{3,2,1,0:T(8,128)S(1)} collective-permute-done((f32[4,2,512,128]{3,2,1,0:T(8,128)S(1)}, f32[4,2,512,128]{3,2,1,0:T(8,128)S(1)}, u32[]{:S(2)}, u32[]{:S(2)}) %collective-permute-start.27) | collective-permute-done | bytes 2097184 | tf_op jit(solution)/shard_map/ppermute | solution.py:85
  1725.5 46.5 %collective-permute-done.29 = f32[4,2,512,128]{3,2,1,0:T(8,128)S(1)} collective-permute-done((f32[4,2,512,128]{3,2,1,0:T(8,128)S(1)}, f32[4,2,512,128]{3,2,1,0:T(8,128)S(1)}, u32[]{:S(2)}, u32[]{:S(2)}) %collective-permute-start.29) | collective-permute-done | bytes 2097184 | tf_op jit(solution)/shard_map/ppermute | solution.py:85
  1773.4 46.7 %collective-permute-done.30 = f32[4,2,512,128]{3,2,1,0:T(8,128)S(1)} collective-permute-done((f32[4,2,512,128]{3,2,1,0:T(8,128)S(1)}, f32[4,2,512,128]{3,2,1,0:T(8,128)S(1)}, u32[]{:S(2)}, u32[]{:S(2)}) %collective-permute-start.30) | collective-permute-done | bytes 2097184 | tf_op jit(solution)/shard_map/ppermute | solution.py:85
  1823.1 90.0 %collective-permute-done.31 = f32[4,2,512,128]{3,2,1,0:T(8,128)S(1)} collective-permute-done((f32[4,2,512,128]{3,2,1,0:T(8,128)S(1)}, f32[4,2,512,128]{3,2,1,0:T(8,128)S(1)}, u32[]{:S(2)}, u32[]{:S(2)}) %collective-permute-start.31) | collective-permute-done | bytes 2097184 | tf_op jit(solution)/shard_map/ppermute | solution.py:85
  1966.6 46.5 %collective-permute-done.33 = f32[4,2,512,128]{3,2,1,0:T(8,128)S(1)} collective-permute-done((f32[4,2,512,128]{3,2,1,0:T(8,128)S(1)}, f32[4,2,512,128]{3,2,1,0:T(8,128)S(1)}, u32[]{:S(2)}, u32[]{:S(2)}) %collective-permute-start.33) | collective-permute-done | bytes 2097184 | tf_op jit(solution)/shard_map/ppermute | solution.py:85
  2014.5 46.8 %collective-permute-done.34 = f32[4,2,512,128]{3,2,1,0:T(8,128)S(1)} collective-permute-done((f32[4,2,512,128]{3,2,1,0:T(8,128)S(1)}, f32[4,2,512,128]{3,2,1,0:T(8,128)S(1)}, u32[]{:S(2)}, u32[]{:S(2)}) %collective-permute-start.34) | collective-permute-done | bytes 2097184 | tf_op jit(solution)/shard_map/ppermute | solution.py:85
  2064.2 90.0 %collective-permute-done.35 = f32[4,2,512,128]{3,2,1,0:T(8,128)S(1)} collective-permute-done((f32[4,2,512,128]{3,2,1,0:T(8,128)S(1)}, f32[4,2,512,128]{3,2,1,0:T(8,128)S(1)}, u32[]{:S(2)}, u32[]{:S(2)}) %collective-permute-start.35) | collective-permute-done | bytes 2097184 | tf_op jit(solution)/shard_map/ppermute | solution.py:85
  2203.4 46.5 %collective-permute-done.37 = f32[4,2,512,128]{3,2,1,0:T(8,128)S(1)} collective-permute-done((f32[4,2,512,128]{3,2,1,0:T(8,128)S(1)}, f32[4,2,512,128]{3,2,1,0:T(8,128)S(1)}, u32[]{:S(2)}, u32[]{:S(2)}) %collective-permute-start.37) | collective-permute-done | bytes 2097184 | tf_op jit(solution)/shard_map/ppermute | solution.py:85
  2250.6 46.8 %collective-permute-done.38 = f32[4,2,512,128]{3,2,1,0:T(8,128)S(1)} collective-permute-done((f32[4,2,512,128]{3,2,1,0:T(8,128)S(1)}, f32[4,2,512,128]{3,2,1,0:T(8,128)S(1)}, u32[]{:S(2)}, u32[]{:S(2)}) %collective-permute-start.38) | collective-permute-done | bytes 2097184 | tf_op jit(solution)/shard_map/ppermute | solution.py:85
  2313.6 78.8 %collective-permute-done.39 = f32[4,2,512,128]{3,2,1,0:T(8,128)} collective-permute-done((f32[4,2,512,128]{3,2,1,0:T(8,128)}, f32[4,2,512,128]{3,2,1,0:T(8,128)}, u32[]{:S(2)}, u32[]{:S(2)}) %collective-permute-start.39) | collective-permute-done | bytes 2097184 | tf_op jit(solution)/shard_map/ppermute | solution.py:85
  2395.6 32.7 %psum.7 = f32[2,11]{1,0:T(2,128)S(1)} all-reduce(f32[2,11]{1,0:T(2,128)S(1)} %concatenate.8735), channel_id=1, replica_groups=mesh['inst'=2,'qy'=4,'qx'=4] {'qy','qx'}, use_global_device_ids=true, to_apply=%region_106.107 | all-reduce | flops 22 | bytes 176 | tf_op jit(solution)/shard_map/psum | solution.py:95
  (2161 shorter events, 791.3 us)
Async XLA Ops:
  16.3 523.5 %copy-start.245 = (f32[2]{0:T(128)}, f32[2]{0:T(128)S(1)}, u32[]{:S(2)}) copy-start(f32[2]{0:T(128)S(1)} %get-tuple-element.31) | copy-start | bytes 28
  16.3 523.5 %copy-start.247 = (f32[2]{0:T(128)}, f32[2]{0:T(128)S(1)}, u32[]{:S(2)}) copy-start(f32[2]{0:T(128)S(1)} %get-tuple-element.3068) | copy-start | bytes 28
  16.3 832.9 %copy-start.81 = (f32[2]{0:T(128)}, f32[2]{0:T(128)S(1)}, u32[]{:S(2)}) copy-start(f32[2]{0:T(128)S(1)} %get-tuple-element.30) | copy-start | bytes 28
  16.3 832.9 %copy-start.236 = (f32[2]{0:T(128)}, f32[2]{0:T(128)S(1)}, u32[]{:S(2)}) copy-start(f32[2]{0:T(128)S(1)} %get-tuple-element.3067) | copy-start | bytes 28
  262.6 2.9 collective-permute-start
  266.5 26.4 %collective-permute-start.1 = (f32[2,2,512,128]{3,1,2,0:T(2,128)S(1)}, f32[2,2,512,128]{3,1,2,0:T(2,128)S(1)}, u32[]{:S(2)}, u32[]{:S(2)}) collective-permute-start(f32[2,2,512,128]{3,1,2,0:T(2,128)S(1)} %pad_maximum_fusion.21), channel_id=1, source_target_pairs={{0,2},{1,3},{2,0},{3,1},{4,6},{5,7},{6,4},{7,5},{8,10},{9,11},{10,... | collective-permute-start | bytes 3145736 | tf_op jit(solution)/shard_map/ppermute | solution.py:70
  294.0 24.7 %collective-permute-start.2 = (f32[2,2,512,128]{3,1,2,0:T(2,128)S(1)}, f32[2,2,512,128]{3,1,2,0:T(2,128)S(1)}, u32[]{:S(2)}, u32[]{:S(2)}) collective-permute-start(f32[2,2,512,128]{3,1,2,0:T(2,128)S(1)} %pad_maximum_fusion.22), channel_id=1, source_target_pairs={{0,4},{4,0},{8,12},{12,8},{1,5},{5,1},{9,13},{13,9},{2,6},{6,2},{1... | collective-permute-start | bytes 3145736 | tf_op jit(solution)/shard_map/ppermute | solution.py:70
  319.8 47.1 %collective-permute-start.3 = (f32[2,2,512,128]{3,1,2,0:T(2,128)S(1)}, f32[2,2,512,128]{3,1,2,0:T(2,128)S(1)}, u32[]{:S(2)}, u32[]{:S(2)}) collective-permute-start(f32[2,2,512,128]{3,1,2,0:T(2,128)S(1)} %pad_maximum_fusion.23), channel_id=1, source_target_pairs={{0,8},{4,12},{8,0},{12,4},{1,9},{5,13},{9,1},{13,5},{2,10},{6,14},... | collective-permute-start | bytes 3145736 | tf_op jit(solution)/shard_map/ppermute | solution.py:70
  596.6 2.7 collective-permute-start.4
  601.2 25.3 %collective-permute-start.5 = (f32[2,2,512,128]{3,1,2,0:T(2,128)S(1)}, f32[2,2,512,128]{3,1,2,0:T(2,128)S(1)}, u32[]{:S(2)}, u32[]{:S(2)}) collective-permute-start(f32[2,2,512,128]{3,1,2,0:T(2,128)S(1)} %pad_maximum_fusion.25), channel_id=1, source_target_pairs={{0,2},{1,3},{2,0},{3,1},{4,6},{5,7},{6,4},{7,5},{8,10},{9,11},{10,... | collective-permute-start | bytes 3145736 | tf_op jit(solution)/shard_map/ppermute | solution.py:70
  627.2 24.4 %collective-permute-start.6 = (f32[2,2,512,128]{3,2,1,0:T(8,128)S(1)}, f32[2,2,512,128]{3,2,1,0:T(8,128)S(1)}, u32[]{:S(2)}, u32[]{:S(2)}) collective-permute-start(f32[2,2,512,128]{3,2,1,0:T(8,128)S(1)} %pad_maximum_fusion.26), channel_id=1, source_target_pairs={{0,4},{4,0},{8,12},{12,8},{1,5},{5,1},{9,13},{13,9},{2,6},{6,2},{1... | collective-permute-start | bytes 3145736 | tf_op jit(solution)/shard_map/ppermute | solution.py:70
  653.1 46.9 %collective-permute-start.7 = (f32[2,2,512,128]{3,1,2,0:T(2,128)S(1)}, f32[2,2,512,128]{3,1,2,0:T(2,128)S(1)}, u32[]{:S(2)}, u32[]{:S(2)}) collective-permute-start(f32[2,2,512,128]{3,1,2,0:T(2,128)S(1)} %pad_maximum_fusion.27), channel_id=1, source_target_pairs={{0,8},{4,12},{8,0},{12,4},{1,9},{5,13},{9,1},{13,5},{2,10},{6,14},... | collective-permute-start | bytes 3145736 | tf_op jit(solution)/shard_map/ppermute | solution.py:70
  855.1 2.7 collective-permute-start.8
  858.1 25.3 %collective-permute-start.9 = (f32[2,2,512,128]{3,2,1,0:T(8,128)S(1)}, f32[2,2,512,128]{3,2,1,0:T(8,128)S(1)}, u32[]{:S(2)}, u32[]{:S(2)}) collective-permute-start(f32[2,2,512,128]{3,2,1,0:T(8,128)S(1)} %pad_maximum_fusion.29), channel_id=1, source_target_pairs={{0,2},{1,3},{2,0},{3,1},{4,6},{5,7},{6,4},{7,5},{8,10},{9,11},{10,... | collective-permute-start | bytes 3145736 | tf_op jit(solution)/shard_map/ppermute | solution.py:70
  883.7 24.4 %collective-permute-start.10 = (f32[2,2,512,128]{3,2,1,0:T(8,128)S(1)}, f32[2,2,512,128]{3,2,1,0:T(8,128)S(1)}, u32[]{:S(2)}, u32[]{:S(2)}) collective-permute-start(f32[2,2,512,128]{3,2,1,0:T(8,128)S(1)} %pad_maximum_fusion.30), channel_id=1, source_target_pairs={{0,4},{4,0},{8,12},{12,8},{1,5},{5,1},{9,13},{13,9},{2,6},{6,2},{1... | collective-permute-start | bytes 3145736 | tf_op jit(solution)/shard_map/ppermute | solution.py:70
  908.4 46.9 %collective-permute-start.11 = (f32[2,2,512,128]{3,2,1,0:T(8,128)S(1)}, f32[2,2,512,128]{3,2,1,0:T(8,128)S(1)}, u32[]{:S(2)}, u32[]{:S(2)}) collective-permute-start(f32[2,2,512,128]{3,2,1,0:T(8,128)S(1)} %pad_maximum_fusion.31), channel_id=1, source_target_pairs={{0,8},{4,12},{8,0},{12,4},{1,9},{5,13},{9,1},{13,5},{2,10},{6,14},... | collective-permute-start | bytes 3145736 | tf_op jit(solution)/shard_map/ppermute | solution.py:70
  974.2 2.7 collective-permute-start.12
  977.3 25.3 %collective-permute-start.13 = (f32[2,2,512,128]{3,2,1,0:T(8,128)S(1)}, f32[2,2,512,128]{3,2,1,0:T(8,128)S(1)}, u32[]{:S(2)}, u32[]{:S(2)}) collective-permute-start(f32[2,2,512,128]{3,2,1,0:T(8,128)S(1)} %pad_maximum_fusion.33), channel_id=1, source_target_pairs={{0,2},{1,3},{2,0},{3,1},{4,6},{5,7},{6,4},{7,5},{8,10},{9,11},{10,... | collective-permute-start | bytes 3145736 | tf_op jit(solution)/shard_map/ppermute | solution.py:70
  1003.0 24.4 %collective-permute-start.14 = (f32[2,2,512,128]{3,2,1,0:T(8,128)S(1)}, f32[2,2,512,128]{3,2,1,0:T(8,128)S(1)}, u32[]{:S(2)}, u32[]{:S(2)}) collective-permute-start(f32[2,2,512,128]{3,2,1,0:T(8,128)S(1)} %pad_maximum_fusion.34), channel_id=1, source_target_pairs={{0,4},{4,0},{8,12},{12,8},{1,5},{5,1},{9,13},{13,9},{2,6},{6,2},{1... | collective-permute-start | bytes 3145736 | tf_op jit(solution)/shard_map/ppermute | solution.py:70
  1027.9 46.9 %collective-permute-start.15 = (f32[2,2,512,128]{3,2,1,0:T(8,128)S(1)}, f32[2,2,512,128]{3,2,1,0:T(8,128)S(1)}, u32[]{:S(2)}, u32[]{:S(2)}) collective-permute-start(f32[2,2,512,128]{3,2,1,0:T(8,128)S(1)} %pad_maximum_fusion.35), channel_id=1, source_target_pairs={{0,8},{4,12},{8,0},{12,4},{1,9},{5,13},{9,1},{13,5},{2,10},{6,14},... | collective-permute-start | bytes 3145736 | tf_op jit(solution)/shard_map/ppermute | solution.py:70
  1092.6 2.7 collective-permute-start.16
  1095.7 25.3 %collective-permute-start.17 = (f32[2,2,512,128]{3,2,1,0:T(8,128)S(1)}, f32[2,2,512,128]{3,2,1,0:T(8,128)S(1)}, u32[]{:S(2)}, u32[]{:S(2)}) collective-permute-start(f32[2,2,512,128]{3,2,1,0:T(8,128)S(1)} %pad_maximum_fusion.37), channel_id=1, source_target_pairs={{0,2},{1,3},{2,0},{3,1},{4,6},{5,7},{6,4},{7,5},{8,10},{9,11},{10,... | collective-permute-start | bytes 3145736 | tf_op jit(solution)/shard_map/ppermute | solution.py:70
  1121.4 24.4 %collective-permute-start.18 = (f32[2,2,512,128]{3,2,1,0:T(8,128)S(1)}, f32[2,2,512,128]{3,2,1,0:T(8,128)S(1)}, u32[]{:S(2)}, u32[]{:S(2)}) collective-permute-start(f32[2,2,512,128]{3,2,1,0:T(8,128)S(1)} %pad_maximum_fusion.38), channel_id=1, source_target_pairs={{0,4},{4,0},{8,12},{12,8},{1,5},{5,1},{9,13},{13,9},{2,6},{6,2},{1... | collective-permute-start | bytes 3145736 | tf_op jit(solution)/shard_map/ppermute | solution.py:70
  1146.5 46.9 %collective-permute-start.19 = (f32[2,2,512,128]{3,2,1,0:T(8,128)S(1)}, f32[2,2,512,128]{3,2,1,0:T(8,128)S(1)}, u32[]{:S(2)}, u32[]{:S(2)}) collective-permute-start(f32[2,2,512,128]{3,2,1,0:T(8,128)S(1)} %pad_maximum_fusion.39), channel_id=1, source_target_pairs={{0,8},{4,12},{8,0},{12,4},{1,9},{5,13},{9,1},{13,5},{2,10},{6,14},... | collective-permute-start | bytes 3145736 | tf_op jit(solution)/shard_map/ppermute | solution.py:70
  1234.3 4.2 collective-permute-start.20
  1239.7 47.7 %collective-permute-start.21 = (f32[4,2,512,128]{3,2,1,0:T(8,128)S(1)}, f32[4,2,512,128]{3,2,1,0:T(8,128)S(1)}, u32[]{:S(2)}, u32[]{:S(2)}) collective-permute-start(f32[4,2,512,128]{3,2,1,0:T(8,128)S(1)} %pad_maximum_fusion.1), channel_id=1, source_target_pairs={{0,2},{1,3},{2,0},{3,1},{4,6},{5,7},{6,4},{7,5},{8,10},{9,11},{10,... | collective-permute-start | bytes 6291464 | tf_op jit(solution)/shard_map/ppermute | solution.py:85
  1288.7 46.9 %collective-permute-start.22 = (f32[4,2,512,128]{3,2,1,0:T(8,128)S(1)}, f32[4,2,512,128]{3,2,1,0:T(8,128)S(1)}, u32[]{:S(2)}, u32[]{:S(2)}) collective-permute-start(f32[4,2,512,128]{3,2,1,0:T(8,128)S(1)} %pad_maximum_fusion.2), channel_id=1, source_target_pairs={{0,4},{4,0},{8,12},{12,8},{1,5},{5,1},{9,13},{13,9},{2,6},{6,2},{1... | collective-permute-start | bytes 6291464 | tf_op jit(solution)/shard_map/ppermute | solution.py:85
  1336.6 91.9 %copy-start.297 = (f32[2]{0:T(128)S(1)}, f32[2]{0:T(128)}, u32[]{:S(2)}) copy-start(f32[2]{0:T(128)} %get-tuple-element.32) | copy-start | bytes 28
  1336.7 91.8 %collective-permute-start.23 = (f32[4,2,512,128]{3,2,1,0:T(8,128)S(1)}, f32[4,2,512,128]{3,2,1,0:T(8,128)S(1)}, u32[]{:S(2)}, u32[]{:S(2)}) collective-permute-start(f32[4,2,512,128]{3,2,1,0:T(8,128)S(1)} %pad_maximum_fusion.3), channel_id=1, source_target_pairs={{0,8},{4,12},{8,0},{12,4},{1,9},{5,13},{9,1},{13,5},{2,10},{6,14},... | collective-permute-start | bytes 6291464 | tf_op jit(solution)/shard_map/ppermute | solution.py:85
  1476.8 4.2 collective-permute-start.24
  1482.2 47.7 %collective-permute-start.25 = (f32[4,2,512,128]{3,2,1,0:T(8,128)S(1)}, f32[4,2,512,128]{3,2,1,0:T(8,128)S(1)}, u32[]{:S(2)}, u32[]{:S(2)}) collective-permute-start(f32[4,2,512,128]{3,2,1,0:T(8,128)S(1)} %pad_maximum_fusion.5), channel_id=1, source_target_pairs={{0,2},{1,3},{2,0},{3,1},{4,6},{5,7},{6,4},{7,5},{8,10},{9,11},{10,... | collective-permute-start | bytes 6291464 | tf_op jit(solution)/shard_map/ppermute | solution.py:85
  1531.2 46.9 %collective-permute-start.26 = (f32[4,2,512,128]{3,2,1,0:T(8,128)S(1)}, f32[4,2,512,128]{3,2,1,0:T(8,128)S(1)}, u32[]{:S(2)}, u32[]{:S(2)}) collective-permute-start(f32[4,2,512,128]{3,2,1,0:T(8,128)S(1)} %pad_maximum_fusion.6), channel_id=1, source_target_pairs={{0,4},{4,0},{8,12},{12,8},{1,5},{5,1},{9,13},{13,9},{2,6},{6,2},{1... | collective-permute-start | bytes 6291464 | tf_op jit(solution)/shard_map/ppermute | solution.py:85
  1579.0 91.9 %copy-start.295 = (f32[2]{0:T(128)S(1)}, f32[2]{0:T(128)}, u32[]{:S(2)}) copy-start(f32[2]{0:T(128)} %get-tuple-element.33) | copy-start | bytes 28
  1579.2 91.8 %collective-permute-start.27 = (f32[4,2,512,128]{3,2,1,0:T(8,128)S(1)}, f32[4,2,512,128]{3,2,1,0:T(8,128)S(1)}, u32[]{:S(2)}, u32[]{:S(2)}) collective-permute-start(f32[4,2,512,128]{3,2,1,0:T(8,128)S(1)} %pad_maximum_fusion.7), channel_id=1, source_target_pairs={{0,8},{4,12},{8,0},{12,4},{1,9},{5,13},{9,1},{13,5},{2,10},{6,14},... | collective-permute-start | bytes 6291464 | tf_op jit(solution)/shard_map/ppermute | solution.py:85
  1718.9 4.2 collective-permute-start.28
  1724.2 47.7 %collective-permute-start.29 = (f32[4,2,512,128]{3,2,1,0:T(8,128)S(1)}, f32[4,2,512,128]{3,2,1,0:T(8,128)S(1)}, u32[]{:S(2)}, u32[]{:S(2)}) collective-permute-start(f32[4,2,512,128]{3,2,1,0:T(8,128)S(1)} %pad_maximum_fusion.9), channel_id=1, source_target_pairs={{0,2},{1,3},{2,0},{3,1},{4,6},{5,7},{6,4},{7,5},{8,10},{9,11},{10,... | collective-permute-start | bytes 6291464 | tf_op jit(solution)/shard_map/ppermute | solution.py:85
  1773.2 46.9 %collective-permute-start.30 = (f32[4,2,512,128]{3,2,1,0:T(8,128)S(1)}, f32[4,2,512,128]{3,2,1,0:T(8,128)S(1)}, u32[]{:S(2)}, u32[]{:S(2)}) collective-permute-start(f32[4,2,512,128]{3,2,1,0:T(8,128)S(1)} %pad_maximum_fusion.10), channel_id=1, source_target_pairs={{0,4},{4,0},{8,12},{12,8},{1,5},{5,1},{9,13},{13,9},{2,6},{6,2},{1... | collective-permute-start | bytes 6291464 | tf_op jit(solution)/shard_map/ppermute | solution.py:85
  1821.2 91.9 %copy-start.289 = (f32[2]{0:T(128)S(1)}, f32[2]{0:T(128)}, u32[]{:S(2)}) copy-start(f32[2]{0:T(128)} %get-tuple-element.34) | copy-start | bytes 28
  1821.3 91.8 %collective-permute-start.31 = (f32[4,2,512,128]{3,2,1,0:T(8,128)S(1)}, f32[4,2,512,128]{3,2,1,0:T(8,128)S(1)}, u32[]{:S(2)}, u32[]{:S(2)}) collective-permute-start(f32[4,2,512,128]{3,2,1,0:T(8,128)S(1)} %pad_maximum_fusion.11), channel_id=1, source_target_pairs={{0,8},{4,12},{8,0},{12,4},{1,9},{5,13},{9,1},{13,5},{2,10},{6,14},... | collective-permute-start | bytes 6291464 | tf_op jit(solution)/shard_map/ppermute | solution.py:85
  1959.9 4.2 collective-permute-start.32
  1965.4 47.7 %collective-permute-start.33 = (f32[4,2,512,128]{3,2,1,0:T(8,128)S(1)}, f32[4,2,512,128]{3,2,1,0:T(8,128)S(1)}, u32[]{:S(2)}, u32[]{:S(2)}) collective-permute-start(f32[4,2,512,128]{3,2,1,0:T(8,128)S(1)} %pad_maximum_fusion.13), channel_id=1, source_target_pairs={{0,2},{1,3},{2,0},{3,1},{4,6},{5,7},{6,4},{7,5},{8,10},{9,11},{10,... | collective-permute-start | bytes 6291464 | tf_op jit(solution)/shard_map/ppermute | solution.py:85
  2014.4 46.9 %collective-permute-start.34 = (f32[4,2,512,128]{3,2,1,0:T(8,128)S(1)}, f32[4,2,512,128]{3,2,1,0:T(8,128)S(1)}, u32[]{:S(2)}, u32[]{:S(2)}) collective-permute-start(f32[4,2,512,128]{3,2,1,0:T(8,128)S(1)} %pad_maximum_fusion.14), channel_id=1, source_target_pairs={{0,4},{4,0},{8,12},{12,8},{1,5},{5,1},{9,13},{13,9},{2,6},{6,2},{1... | collective-permute-start | bytes 6291464 | tf_op jit(solution)/shard_map/ppermute | solution.py:85
  2062.3 91.9 %copy-start.292 = (f32[2]{0:T(128)S(1)}, f32[2]{0:T(128)}, u32[]{:S(2)}) copy-start(f32[2]{0:T(128)} %get-tuple-element.35) | copy-start | bytes 28
  2062.5 91.8 %collective-permute-start.35 = (f32[4,2,512,128]{3,2,1,0:T(8,128)S(1)}, f32[4,2,512,128]{3,2,1,0:T(8,128)S(1)}, u32[]{:S(2)}, u32[]{:S(2)}) collective-permute-start(f32[4,2,512,128]{3,2,1,0:T(8,128)S(1)} %pad_maximum_fusion.15), channel_id=1, source_target_pairs={{0,8},{4,12},{8,0},{12,4},{1,9},{5,13},{9,1},{13,5},{2,10},{6,14},... | collective-permute-start | bytes 6291464 | tf_op jit(solution)/shard_map/ppermute | solution.py:85
  2197.2 4.2 collective-permute-start.36
  2202.1 47.7 %collective-permute-start.37 = (f32[4,2,512,128]{3,2,1,0:T(8,128)S(1)}, f32[4,2,512,128]{3,2,1,0:T(8,128)S(1)}, u32[]{:S(2)}, u32[]{:S(2)}) collective-permute-start(f32[4,2,512,128]{3,2,1,0:T(8,128)S(1)} %pad_maximum_fusion.17), channel_id=1, source_target_pairs={{0,2},{1,3},{2,0},{3,1},{4,6},{5,7},{6,4},{7,5},{8,10},{9,11},{10,... | collective-permute-start | bytes 6291464 | tf_op jit(solution)/shard_map/ppermute | solution.py:85
  2250.6 46.9 %collective-permute-start.38 = (f32[4,2,512,128]{3,2,1,0:T(8,128)S(1)}, f32[4,2,512,128]{3,2,1,0:T(8,128)S(1)}, u32[]{:S(2)}, u32[]{:S(2)}) collective-permute-start(f32[4,2,512,128]{3,2,1,0:T(8,128)S(1)} %pad_maximum_fusion.18), channel_id=1, source_target_pairs={{0,4},{4,0},{8,12},{12,8},{1,5},{5,1},{9,13},{13,9},{2,6},{6,2},{1... | collective-permute-start | bytes 6291464 | tf_op jit(solution)/shard_map/ppermute | solution.py:85
  2300.7 91.7 %collective-permute-start.39 = (f32[4,2,512,128]{3,2,1,0:T(8,128)}, f32[4,2,512,128]{3,2,1,0:T(8,128)}, u32[]{:S(2)}, u32[]{:S(2)}) collective-permute-start(f32[4,2,512,128]{3,2,1,0:T(8,128)} %pad_maximum_fusion.19), channel_id=1, source_target_pairs={{0,8},{4,12},{8,0},{12,4},{1,9},{5,13},{9,1},{13,5},{2,10},{6,14},... | collective-permute-start | bytes 6291464 | tf_op jit(solution)/shard_map/ppermute | solution.py:85
  (369 other events, 4610.6 us)
where the time goes:
time: 2440 us; the launch traced here: 2430 us
  waiting for transfers between devices  1400 us (57%)
  other arithmetic  601 us (25%)
  local copies, waits for them, and re-layouts  349 us (14%)
  starting transfers between devices  38.4 us (2%)
  blocking collectives  32.7 us (1%)
    ppermute x20, waiting for transfers between devices, device_fn(): partner = lax.ppermute(jnp.stack(list(four_amps)), axis_name, pair_list)  926 us
    ppermute x20, waiting for transfers between devices, device_fn(): partner = lax.ppermute(jnp.stack([psi_re, psi_im]), axis_name, pair_list)  471 us
    concatenate x132, local copies, waits for them, and re-layouts, flip_grid(): jnp.roll(amplitudes, shift, axis=axis_pos)  151 us
    reduce_sum x95, other arithmetic, inverse_step(): term = jnp.sum(lam_re * partner[1] - lam_im * partner[0], axis=(1, 2))  135 us
    add x41, other arithmetic, device_fn(): cos_b * psi_re + sin_b * flip_im  126 us
    sub x41, other arithmetic, device_fn(): cos_b * psi_im - sin_b * flip_re  107 us
    slice x689, local copies, waits for them, and re-layouts, flip_grid(): jnp.roll(amplitudes, shift, axis=axis_pos)  83.7 us
    concatenate x58, local copies, waits for them, and re-layouts, flip_grid(): jnp.roll(amplitudes, -shift, axis=axis_pos)  72.5 us
  transfers between devices with their start and end apart: 40, of which 40 were waited for; matrix products, arithmetic and copies ran while one was open for 1% of the time, Pallas kernels for 0%

commit v1 on v0

v1 whole, which is shorter than its diff:
```python
import functools
import jax
import jax.numpy as jnp
from jax import lax
from jax.experimental import pallas as pl
from jax.experimental.pallas import tpu as pltpu
from jax.sharding import PartitionSpec as P

F32 = jnp.float32
BF16 = jnp.bfloat16
LAYERS = 5
LOCAL_QUBITS = 19
CHUNK = 64
NUM_CHUNKS = 256 // CHUNK
NUM_ACC = 16
MESH = pl.DeviceIdType.MESH
HOMES = ((1, 0), (2, 2))


def sincos(x):
    magic = 12582912.0
    k = (x * 0.6366197723675814 + magic) - magic
    r = ((x - k * 1.5703125) - k * 4.837512969970703125e-4) - k * 7.54978995489188216e-8
    z = r * r
    sin_r = ((-1.9515295891e-4 * z + 8.3321608736e-3) * z - 1.6666654611e-1) * (z * r) + r
    cos_r = ((2.443315711809948e-5 * z - 1.388731625493765e-3) * z + 4.166664568298827e-2) * (z * z) - (0.5 * z - 1.0)
    quad = k.astype(jnp.int32)
    odd = (quad & 1) == 1
    sin_x = jnp.where(odd, cos_r, sin_r)
    cos_x = jnp.where(odd, sin_r, cos_r)
    sin_x = jnp.where((quad & 2) == 2, -sin_x, sin_x)
    cos_x = jnp.where(((quad + 1) & 2) == 2, -cos_x, cos_x)
    return sin_x, cos_x


def split3(x):
    a = x.astype(BF16)
    r = x - a.astype(F32)
    b = r.astype(BF16)
    c = (r - b.astype(F32)).astype(BF16)
    return a, b, c


def butterfly8(v):
    for step in (4, 2, 1):
        out = list(v)
        for i in range(8):
            if not i & step:
                out[i] = v[i] + v[i + step]
                out[i + step] = v[i] - v[i + step]
        v = out
    return v


def popcount_tile(shape):
    sub = lax.broadcasted_iota(jnp.int32, shape, 0)
    lane = lax.broadcasted_iota(jnp.int32, shape, 1)
    total = jnp.zeros(shape, jnp.int32)
    for b in range(3):
        total = total + ((sub >> b) & 1)
    for b in range(7):
        total = total + ((lane >> b) & 1)
    return total.astype(F32)


def fold(x):
    return jnp.sum(x.reshape(-1, 8, 128), axis=0)


def dot3(lhs, rhs):
    return sum(jnp.dot(a, b, preferred_element_type=F32) for a, b in zip(lhs, rhs))


def cols_of(ct):
    return pl.ds(ct * 128, 128)


def rotate(values, cos_b, sin_b):
    kr, ki, orr, oi = values
    return (cos_b * kr + sin_b * oi, cos_b * ki - sin_b * orr, cos_b * orr + sin_b * ki, cos_b * oi - sin_b * kr)


def groups(i):
    for g in range(CHUNK // 16):
        for ct in range(2):
            start = pl.multiple_of(i * CHUNK + g * 16, 16)
            cost_start = pl.multiple_of(ct * 256 + i * CHUNK + g * 16, 16)
            yield pl.ds(g * 16, 16), pl.ds(start, 16), cols_of(ct), pl.ds(cost_start, 16)


def loop(count, body):
    def step(n, carry):
        body(n)
        return carry
    lax.fori_loop(0, count, step, 0)


def kernel(cost, gamma, beta, had, out, stash, keep, other, cc, tab, saved, hat, diag, rot, acc,
           parts, wide, big, mine, res, c_send, c_recv, f_send, f_recv, x_send, x_recv, h_out, h_in, r_send, r_recv, credit):
    inst = lax.axis_index('inst')
    qy = lax.axis_index('qy')
    qx = lax.axis_index('qx')
    core = lax.rem(qx, 2)
    my_set = qx // 2
    active = qy == my_set + 1
    partner = (inst, qy, qx + 1 - 2 * core)
    kind = lax.rem(qy // 2 + qy, 2)

    def cost_copy(s):
        home_y, home_x = HOMES[s]
        return pltpu.make_async_remote_copy(
            src_ref=cost, dst_ref=cc.at[kind, qx], send_sem=c_send.at[s], recv_sem=c_recv.at[kind, qx],
            device_id=(inst, home_y, home_x + qy // 2), device_id_type=MESH)

    def is_self(s):
        home_y, home_x = HOMES[s]
        return (qy == home_y) & (qx == home_x + qy // 2)

    for s in range(2):
        @pl.when(is_self(s))
        def _():
            pltpu.make_async_copy(cost, cc.at[kind, qx], c_recv.at[kind, qx]).start()

        @pl.when(jnp.logical_not(is_self(s)))
        def _():
            cost_copy(s).start()

    def cost_arrived(which, j):
        pltpu.make_async_copy(cost, cc.at[which, j], c_recv.at[which, j]).wait()

    def forward_copy(j):
        return pltpu.make_async_remote_copy(
            src_ref=cc.at[1, j], dst_ref=cc.at[2, j], send_sem=f_send.at[j], recv_sem=f_recv.at[j],
            device_id=partner, device_id_type=MESH)

    def exchange(parity, i):
        rows = pl.ds(pl.multiple_of(i * CHUNK, CHUNK), CHUNK)
        return pltpu.make_async_remote_copy(
            src_ref=other.at[1 - parity, :, :, rows, :], dst_ref=other.at[parity, :, :, rows, :],
            send_sem=x_send.at[parity, i], recv_sem=x_recv.at[parity, i],
            device_id=partner, device_id_type=MESH)

    def release(i):
        pl.semaphore_signal(credit.at[i], inc=1, device_id=partner, device_id_type=MESH)

    def send(parity, i, first=None):
        if first is None:
            pl.semaphore_wait(credit.at[i], 1)
        else:
            @pl.when(jnp.logical_not(first))
            def _():
                pl.semaphore_wait(credit.at[i], 1)
        exchange(parity, i).start()

    def stash_out(n):
        return pltpu.make_async_copy(hat.at[lax.rem(n, 2)], stash.at[n], h_out.at[lax.rem(n, 2)])

    def stash_in(n):
        return pltpu.make_async_copy(stash.at[n], hat.at[lax.rem(n, 2)], h_in.at[lax.rem(n, 2)])

    def put_parts(t, rows, cols, x):
        for p, piece in enumerate(split3(x)):
            parts[p, t, rows, cols] = piece

    def right_multiply(write):
        h = had[...]
        for t in range(0, 16, 4):
            lhs = [parts[p, t:t + 4].reshape(4 * CHUNK, 256) for p in range(3)]
            write(t, dot3(lhs, (h, h, h)).reshape(4, CHUNK, 256))

    def state_write(par, i):
        rows = pl.ds(pl.multiple_of(i * CHUNK, CHUNK), CHUNK)

        def write(t, value):
            comp, half = t // 8, (t // 4) % 2
            if half == 0:
                keep[comp, :, rows, :] = value
            else:
                other[par, comp, :, rows, :] = value
        return write

    def big_write(t, value):
        big[t:t + 4] = value

    def load_state(par, rows, cols, j):
        return (keep[0, j, rows, cols], keep[1, j, rows, cols],
                other[par, 0, j, rows, cols], other[par, 1, j, rows, cols])

    def store_state(par, rows, cols, j, values):
        keep[0, j, rows, cols] = values[0]
        keep[1, j, rows, cols] = values[1]
        other[par, 0, j, rows, cols] = values[2]
        other[par, 1, j, rows, cols] = values[3]

    def spread(re, im, local_rows, cols):
        for comp, v in enumerate((butterfly8(re), butterfly8(im))):
            for t in range(8):
                put_parts(comp * 8 + t, local_rows, cols, v[t])

    def gather_big(local_rows, cols):
        re = butterfly8([big[t, local_rows, cols] for t in range(8)])
        im = butterfly8([big[8 + t, local_rows, cols] for t in range(8)])
        return re, im

    def inverse_chunk(par, i):
        for g in range(CHUNK // 16):
            rows = pl.ds(pl.multiple_of(i * CHUNK + g * 16, 16), 16)
            for ct in range(2):
                for j in range(4):
                    v = load_state(par, rows, cols_of(ct), j)
                    for t, x in zip((j, 8 + j, 4 + j, 12 + j), v):
                        put_parts(t, pl.ds(g * 16, 16), cols_of(ct), x)
        right_multiply(big_write)

    def middle(layer, par, forward):
        h = had[...]
        slot = lax.rem(layer, 2)

        def block(j, total, half):
            n = half * 4 + j
            bits = half + j // 2 + lax.rem(j, 2)
            for comp in range(2):
                src = keep[comp, j] if half == 0 else other[par, comp, j]
                wide[comp] = dot3((h, h, h), split3(src))
            for g in range(16):
                rows = pl.ds(g * 16, 16)
                for ct in range(2):
                    cols = cols_of(ct)
                    q0 = bin(2 * g).count('1') + ct
                    q1 = bin(2 * g + 1).count('1') + ct

                    def pick(m):
                        return jnp.concatenate([diag[layer, m, bits + q0], diag[layer, m, bits + q1]], axis=0)
                    re, im = wide[0, rows, cols], wide[1, rows, cols]
                    dc, ds = pick(0), pick(1)
                    if forward:
                        re, im = re * dc + im * ds, im * dc - re * ds
                        hat[slot, 0, n, rows, cols] = re
                        hat[slot, 1, n, rows, cols] = im
                    else:
                        term = re * hat[slot, 1, n, rows, cols] - im * hat[slot, 0, n, rows, cols]
                        total = total + fold(term * pick(2))
                        re, im = re * dc - im * ds, im * dc + re * ds
                    wide[0, rows, cols] = re
                    wide[1, rows, cols] = im
            for comp in range(2):
                value = dot3((h, h, h), split3(wide[comp]))
                if half == 0:
                    keep[comp, j] = value
                else:
                    other[par, comp, j] = value
            return total

        def body(j, total):
            return block(j, block(j, total, 0), 1)
        return lax.fori_loop(0, 4, body, jnp.zeros((8, 128), F32))

    def tables():
        pop = popcount_tile((8, 128))
        for layer in range(LAYERS):
            half_angle = jnp.full((8, 128), 0.5, F32) * beta[my_set, layer]

            def entry(q):
                weight = (LOCAL_QUBITS - 2 * q).astype(F32) - 2.0 * pop
                sin_d, cos_d = sincos(half_angle * weight)
                diag[layer, 0, q] = cos_d * (2.0 ** -LOCAL_QUBITS)
                diag[layer, 1, q] = sin_d * (2.0 ** -LOCAL_QUBITS)
                diag[layer, 2, q] = weight
            loop(10, entry)
            sin_h, cos_h = sincos(jnp.concatenate([half_angle, half_angle], axis=0))
            rot[layer + 1, 0] = cos_h
            rot[layer + 1, 1] = sin_h
        rot[0, 0] = jnp.ones((16, 128), F32)
        rot[0, 1] = jnp.zeros((16, 128), F32)
        acc[...] = jnp.zeros((NUM_ACC, 8, 128), F32)

        def init(r):
            rows = pl.ds(pl.multiple_of(r * 16, 16), 16)
            for j in range(4):
                start = jnp.full((16, 256), 2.0 ** -10, F32)
                zero = jnp.zeros((16, 256), F32)
                keep[0, j, rows, :] = start
                keep[1, j, rows, :] = zero
                other[0, 0, j, rows, :] = start
                other[0, 1, j, rows, :] = zero
        loop(16, init)

    def fill(layer, which, half, j):
        def rows_body(r):
            start = pl.multiple_of(r * 32, 32)
            for ct in range(2):
                cost_rows = pl.ds(pl.multiple_of(ct * 256 + start, 32), 32)
                sin_p, cos_p = sincos(gamma[my_set, layer] * cc[which, j, cost_rows, :])
                tab[layer, 0, half * 4 + j, pl.ds(start, 32), cols_of(ct)] = cos_p
                tab[layer, 1, half * 4 + j, pl.ds(start, 32), cols_of(ct)] = sin_p
        loop(8, rows_body)

    def arrive(j):
        cost_arrived(1, j)
        forward_copy(j).start()
        loop(3, lambda n: fill(2 * n, 1, 1, j))
        cost_arrived(0, j)
        loop(LAYERS, lambda n: fill(n, 0, 0, j))
        forward_copy(j).wait()
        loop(2, lambda n: fill(2 * n + 1, 2, 1, j))

    def forward_layer(layer):
        par = lax.rem(layer, 2)

        def alpha(i):
            @pl.when(layer > 0)
            def _():
                exchange(par, i).wait()
                release(i)
            cos_b, sin_b = rot[layer, 0], rot[layer, 1]
            for local_rows, rows, cols, _c in groups(i):
                re, im = [None] * 8, [None] * 8
                for j in range(4):
                    v = rotate(load_state(par, rows, cols, j), cos_b, sin_b)
                    for half in range(2):
                        n = half * 4 + j
                        pr, pi = v[2 * half], v[2 * half + 1]
                        saved[layer, 0, n, rows, cols] = pr
                        saved[layer, 1, n, rows, cols] = pi
                        c, s = tab[layer, 0, n, rows, cols], tab[layer, 1, n, rows, cols]
                        re[n], im[n] = pr * c + pi * s, pi * c - pr * s
                spread(re, im, local_rows, cols)
            right_multiply(state_write(par, i))
        loop(NUM_CHUNKS, alpha)

        @pl.when((layer >= 2))
        def _():
            stash_out(layer - 2).wait()
        middle(layer, par, True)

        @pl.when(layer < 3)
        def _():
            stash_out(layer).start()

        def gamma_sweep(i):
            inverse_chunk(par, i)
            for local_rows, rows, cols, _c in groups(i):
                re, im = gather_big(local_rows, cols)
                for j in range(4):
                    store_state(par, rows, cols, j, (re[j], im[j], re[4 + j], im[4 + j]))

            @pl.when(i > 0)
            def _():
                send(1 - par, i - 1, layer == 0)
        loop(NUM_CHUNKS, gamma_sweep)
        send(1 - par, NUM_CHUNKS - 1, layer == 0)

    def final(i):
        exchange(1, i).wait()
        release(i)
        energy = jnp.zeros((8, 128), F32)
        grad = jnp.zeros((8, 128), F32)
        cos_b, sin_b = rot[LAYERS, 0], rot[LAYERS, 1]
        for local_rows, rows, cols, crows in groups(i):
            for j in range(4):
                kr, ki, orr, oi = rotate(load_state(1, rows, cols, j), cos_b, sin_b)
                ck, co = cc[0, j, crows, :], cc[2, j, crows, :]
                lam = (ck * kr, ck * ki, co * orr, co * oi)
                energy = energy + fold(lam[0] * kr + lam[1] * ki + lam[2] * orr + lam[3] * oi)
                grad = grad + fold((ck - co) * (kr * oi - ki * orr))
                store_state(1, rows, cols, j, rotate(lam, cos_b, -sin_b))
        acc[0] = acc[0] + energy
        acc[2 * LAYERS] = acc[2 * LAYERS] + grad

        @pl.when(i > 0)
        def _():
            send(0, i - 1)

    def backward_layer(step):
        layer = LAYERS - 1 - step
        par = lax.rem(layer, 2)

        def alpha(i):
            exchange(par, i).wait()

            @pl.when(layer > 0)
            def _():
                release(i)
            for local_rows, rows, cols, _c in groups(i):
                v = [load_state(par, rows, cols, j) for j in range(4)]
                re = [v[j][0] for j in range(4)] + [v[j][2] for j in range(4)]
                im = [v[j][1] for j in range(4)] + [v[j][3] for j in range(4)]
                spread(re, im, local_rows, cols)
            right_multiply(state_write(par, i))
        loop(NUM_CHUNKS, alpha)

        @pl.when(layer < 3)
        def _():
            stash_in(layer).wait()
        total = middle(layer, par, False)
        acc[LAYERS + 1 + layer] = acc[LAYERS + 1 + layer] + total

        @pl.when(layer >= 2)
        def _():
            stash_in(layer - 2).start()

        def gamma_sweep(i):
            inverse_chunk(par, i)
            g_sum = jnp.zeros((8, 128), F32)
            b_sum = jnp.zeros((8, 128), F32)
            cos_b, sin_b = rot[layer, 0], rot[layer, 1]
            for local_rows, rows, cols, crows in groups(i):
                re, im = gather_big(local_rows, cols)
                for j in range(4):
                    lam, psi = [], []
                    for half in range(2):
                        n = half * 4 + j
                        c, s = tab[layer, 0, n, rows, cols], tab[layer, 1, n, rows, cols]
                        lr, li = re[n] * c - im[n] * s, im[n] * c + re[n] * s
                        pr, pi = saved[layer, 0, n, rows, cols], saved[layer, 1, n, rows, cols]
                        cost_n = cc[0, j, crows, :] if half == 0 else cc[1 + par, j, crows, :]
                        g_sum = g_sum + fold(cost_n * (lr * pi - li * pr))
                        lam += [lr, li]
                        psi += [pr, pi]
                    b_sum = b_sum + fold(lam[0] * psi[3] - lam[1] * psi[2] + lam[2] * psi[1] - lam[3] * psi[0])
                    store_state(par, rows, cols, j, rotate(lam, cos_b, -sin_b))
            acc[1 + layer] = acc[1 + layer] + 2.0 * g_sum

            @pl.when(layer > 0)
            def _():
                acc[LAYERS + layer] = acc[LAYERS + layer] + b_sum

            @pl.when((i > 0) & (layer > 0))
            def _():
                send(1 - par, i - 1)
        loop(NUM_CHUNKS, gamma_sweep)

        @pl.when(layer > 0)
        def _():
            send(1 - par, NUM_CHUNKS - 1)

    def result_copy(a, b):
        return pltpu.make_async_remote_copy(
            src_ref=mine, dst_ref=res.at[qx], send_sem=r_send.at[a * 4 + b], recv_sem=r_recv.at[qx],
            device_id=(inst, a, b), device_id_type=MESH)

    def others(fn):
        for a in range(4):
            for b in range(4):
                @pl.when((qy != a) | (qx != b))
                def _():
                    fn(result_copy(a, b))

    @pl.when(active)
    def _():
        tables()
        loop(4, arrive)
        loop(LAYERS, forward_layer)
        loop(NUM_CHUNKS, final)
        send(0, NUM_CHUNKS - 1)
        loop(LAYERS, backward_layer)
        mine[...] = jnp.sum(acc[...], axis=1)
        res[qx] = mine[...]
        others(lambda copy: copy.start())

    for slot in range(4):
        @pl.when(jnp.logical_not(active & (qx == slot)))
        def _():
            pltpu.make_async_remote_copy(
                src_ref=mine, dst_ref=res.at[slot], send_sem=r_send.at[0], recv_sem=r_recv.at[slot],
                device_id=partner, device_id_type=MESH).wait_recv()

    for s in range(2):
        total = jnp.sum(res[2 * s] + res[2 * s + 1], axis=1, keepdims=True)
        out[s] = jnp.broadcast_to(total, (NUM_ACC, 128))

    for s in range(2):
        @pl.when(jnp.logical_not(is_self(s)))
        def _():
            cost_copy(s).wait_send()

    @pl.when(active)
    def _():
        others(lambda copy: copy.wait_send())


def hadamard():
    index = jnp.arange(256, dtype=jnp.int32)
    both = index[:, None] & index[None, :]
    parity = jnp.zeros((256, 256), jnp.int32)
    for b in range(8):
        parity = parity ^ ((both >> b) & 1)
    return (1 - 2 * parity).astype(BF16)


def solution(mesh):
    def device_fn(cost, gamma, beta):
        vmem = pltpu.VMEM
        dma = pltpu.SemaphoreType.DMA
        tile = (256, 256)
        out, _ = pl.pallas_call(
            kernel,
            out_shape=(jax.ShapeDtypeStruct((2, NUM_ACC, 128), F32), jax.ShapeDtypeStruct((3, 2, 8) + tile, F32)),
            in_specs=[pl.BlockSpec(memory_space=pl.ANY), pl.BlockSpec(memory_space=pltpu.SMEM),
                      pl.BlockSpec(memory_space=pltpu.SMEM), pl.BlockSpec(memory_space=pltpu.VMEM)],
            out_specs=(pl.BlockSpec(memory_space=pltpu.VMEM), pl.BlockSpec(memory_space=pl.ANY)),
            scratch_shapes=[
                vmem((2, 4) + tile, F32),
                vmem((2, 2, 4) + tile, F32),
                vmem((3, 4, 512, 128), F32),
                vmem((LAYERS, 2, 8) + tile, F32),
                vmem((LAYERS, 2, 8) + tile, F32),
                vmem((2, 2, 8) + tile, F32),
                vmem((LAYERS, 3, 10, 8, 128), F32),
                vmem((LAYERS + 1, 2, 16, 128), F32),
                vmem((NUM_ACC, 8, 128), F32),
                vmem((3, 16, CHUNK, 256), BF16),
                vmem((2,) + tile, F32),
                vmem((16, CHUNK, 256), F32),
                vmem((NUM_ACC, 128), F32),
                vmem((4, NUM_ACC, 128), F32),
                dma((2,)), dma((2, 4)), dma((4,)), dma((4,)), dma((2, NUM_CHUNKS)), dma((2, NUM_CHUNKS)),
                dma((2,)), dma((2,)), dma((16,)), dma((4,)), pltpu.SemaphoreType.REGULAR((NUM_CHUNKS,)),
            ],
            compiler_params=pltpu.CompilerParams(has_side_effects=True, vmem_limit_bytes=67043328),
        )(cost.reshape(512, 128), gamma, beta, hadamard())
        return out[:, 0, 0], out[:, 1:1 + 2 * LAYERS, 0]

    cost_spec = P(('inst', 'qy', 'qx'))
    angle_spec = P('inst', None)
    return jax.shard_map(device_fn, mesh=mesh, in_specs=(cost_spec, angle_spec, angle_spec), out_specs=(P('inst'), angle_spec), check_vma=False)
```

time: 2440 us -> 195 us (0.08)
  waiting for transfers between devices: 1400 us -> 0 us
  other arithmetic: 601 us -> 0.89 us
  local copies, waits for them, and re-layouts: 349 us -> 2.67 us
  Pallas kernels: 0 us -> 191 us
  starting transfers between devices: 38.4 us -> 0 us
  blocking collectives: 32.7 us -> 0 us
    ppermute x40 -> x0, waiting for transfers between devices: 1400 us -> none  [the longest x20 926 us: device_fn(): partner = lax.ppermute(jnp.stack(list(four_amps)), axis_name, pair_list)]
    concatenate x191 -> x0, local copies, waits for them, and re-layouts: 224 us -> none  [the longest x132 151 us: flip_grid(): jnp.roll(amplitudes, shift, axis=axis_pos)]
    pallas_call x0 -> x1, Pallas kernels: none -> 191 us  [device_fn(): pl.pallas_call(kernel, out_shape=(jax.ShapeDtypeStruct((2, NUM_ACC, 128),...]
    add x105 -> x0, other arithmetic: 165 us -> none  [the longest x41 126 us: device_fn(): cos_b * psi_re + sin_b * flip_im]
    sub x84 -> x0, other arithmetic: 141 us -> none  [the longest x41 107 us: device_fn(): cos_b * psi_im - sin_b * flip_re]
    reduce_sum x96 -> x0, other arithmetic: 139 us -> none  [the longest x95 135 us: inverse_step(): term = jnp.sum(lam_re * partner[1] - lam_im * partner[0], axis=(1, 2))]
    mul x30 -> x0, other arithmetic: 137 us -> none  [the longest x7 41.9 us: device_fn(): sin_b * flip_im]
    slice x776 -> x2, local copies, waits for them, and re-layouts: 112 us -> 2.67 us  [device_fn(): return (out[:, 0, 0], out[:, 1:1 + 2 * LAYERS, 0])]
  transfers between devices with their start and end apart: 40 -> 0, of which waited for: 40 -> 0; matrix products, arithmetic and copies ran while one was open for 1% -> 0% of each run, Pallas kernels for 0% -> 0%
where the time goes in v1:
time: 195 us
  Pallas kernels  191 us (98%)
  local copies, waits for them, and re-layouts  2.67 us (1%)
    pallas_call x1, Pallas kernels, device_fn(): pl.pallas_call(kernel, out_shape=(jax.ShapeDtypeStruct((2, NUM_ACC, 128),...  191 us

profile of v1, /device:TPU:0, one launch (start us, length us, event | category | flops | bytes accessed | tf_op | source)
XLA Modules:
  0.0 195.2 jit_solution(12813365033997718137)
XLA Ops:
  0.6 0.9 subtract_convert_fusion.had
  1.5 191.0 %shard_map.50 = (f32[2,16,128]{2,1,0:T(8,128)}, f32[3,2,8,256,256]{4,3,2,1,0:T(8,128)}) custom-call(f32[512,128]{1,0:T(8,128)} %bitcast.1, f32[2,5]{1,0:T(2,128)} %gamma.1, f32[2,5]{1,0:T(2,128)} %beta.1, bf16[256,256]{1,0:T(8,128)(2,1)} %subtract_convert_fusion.had), custom_call_target="tpu_custom_call" | custom-call | tf_op jit(solution)/shard_map/pallas_call | solution.py:496
  192.5 1.3 slice_reduce_fusion.1
  193.8 1.4 slice_reduce_fusion

commit v2 on v1

--- a/solution.py
+++ b/solution.py
@@ -1,4 +1,5 @@
-import functools
+import math
+import numpy as np
 import jax
 import jax.numpy as jnp
 from jax import lax
@@ -11,26 +12,23 @@
 LAYERS = 5
 LOCAL_QUBITS = 19
 CHUNK = 64
+STRIP = 64
 NUM_CHUNKS = 256 // CHUNK
 NUM_ACC = 16
+SIN = (3.14159265353629, -5.16771276462444, 2.550163318944362, -0.5992521977957433, 0.08205040168394097, -0.00702838621010907)
+COS = (0.9999999997799045, -4.9348021370788056, 4.058709159555753, -1.3352120030448535, 0.23493731379172217, -0.024396324310603436)
 MESH = pl.DeviceIdType.MESH
 HOMES = ((1, 0), (2, 2))
 
 
-def sincos(x):
+def sincos_turns(u):
     magic = 12582912.0
-    k = (x * 0.6366197723675814 + magic) - magic
-    r = ((x - k * 1.5703125) - k * 4.837512969970703125e-4) - k * 7.54978995489188216e-8
-    z = r * r
-    sin_r = ((-1.9515295891e-4 * z + 8.3321608736e-3) * z - 1.6666654611e-1) * (z * r) + r
-    cos_r = ((2.443315711809948e-5 * z - 1.388731625493765e-3) * z + 4.166664568298827e-2) * (z * z) - (0.5 * z - 1.0)
-    quad = k.astype(jnp.int32)
-    odd = (quad & 1) == 1
-    sin_x = jnp.where(odd, cos_r, sin_r)
-    cos_x = jnp.where(odd, sin_r, cos_r)
-    sin_x = jnp.where((quad & 2) == 2, -sin_x, sin_x)
-    cos_x = jnp.where(((quad + 1) & 2) == 2, -cos_x, cos_x)
-    return sin_x, cos_x
+    f = u - ((u + magic) - magic)
+    z = f * f
+    sin_h = f * (SIN[0] + z * (SIN[1] + z * (SIN[2] + z * (SIN[3] + z * (SIN[4] + z * SIN[5])))))
+    cos_h = COS[0] + z * (COS[1] + z * (COS[2] + z * (COS[3] + z * (COS[4] + z * COS[5]))))
+    twice = sin_h + sin_h
+    return twice * cos_h, 1.0 - twice * sin_h
 
 
 def split3(x):
@@ -67,10 +65,6 @@
     return jnp.sum(x.reshape(-1, 8, 128), axis=0)
 
 
-def dot3(lhs, rhs):
-    return sum(jnp.dot(a, b, preferred_element_type=F32) for a, b in zip(lhs, rhs))
-
-
 def cols_of(ct):
     return pl.ds(ct * 128, 128)
 
@@ -96,7 +90,7 @@
 
 
 def kernel(cost, gamma, beta, had, out, stash, keep, other, cc, tab, saved, hat, diag, rot, acc,
-           parts, wide, big, mine, res, c_send, c_recv, f_send, f_recv, x_send, x_recv, h_out, h_in, r_send, r_recv, credit):
+           wide, flip, big, mine, res, c_send, c_recv, f_send, f_recv, x_send, x_recv, h_out, h_in, r_send, r_recv, credit):
     inst = lax.axis_index('inst')
     qy = lax.axis_index('qy')
     qx = lax.axis_index('qx')
@@ -158,29 +152,31 @@
     def stash_in(n):
         return pltpu.make_async_copy(stash.at[n], hat.at[lax.rem(n, 2)], h_in.at[lax.rem(n, 2)])
 
-    def put_parts(t, rows, cols, x):
-        for p, piece in enumerate(split3(x)):
-            parts[p, t, rows, cols] = piece
-
-    def right_multiply(write):
+    def multiply(strips):
         h = had[...]
-        for t in range(0, 16, 4):
-            lhs = [parts[p, t:t + 4].reshape(4 * CHUNK, 256) for p in range(3)]
-            write(t, dot3(lhs, (h, h, h)).reshape(4, CHUNK, 256))
-
-    def state_write(par, i):
+        for read, write in strips:
+            parts = jnp.dot(jnp.concatenate(split3(read()), axis=0), h, preferred_element_type=F32)
+            write(parts[0:STRIP] + parts[STRIP:2 * STRIP] + parts[2 * STRIP:3 * STRIP])
+
+    def state_tile(par, t, rows):
+        comp, half, j = t // 8, (t // 4) % 2, t % 4
+        return keep.at[comp, j, rows, :] if half == 0 else other.at[par, comp, j, rows, :]
+
+    def pair(src, dst):
+        def read():
+            return src[...]
+
+        def write(value):
+            dst[...] = value
+        return read, write
+
+    def to_state(par, i):
         rows = pl.ds(pl.multiple_of(i * CHUNK, CHUNK), CHUNK)
-
-        def write(t, value):
-            comp, half = t // 8, (t // 4) % 2
-            if half == 0:
-                keep[comp, :, rows, :] = value
-            else:
-                other[par, comp, :, rows, :] = value
-        return write
-
-    def big_write(t, value):
-        big[t:t + 4] = value
+        multiply([pair(big.at[t], state_tile(par, t, rows)) for t in range(16)])
+
+    def from_state(par, i):
+        rows = pl.ds(pl.multiple_of(i * CHUNK, CHUNK), CHUNK)
+        multiply([pair(state_tile(par, t, rows), big.at[t]) for t in range(16)])
 
     def load_state(par, rows, cols, j):
         return (keep[0, j, rows, cols], keep[1, j, rows, cols],
@@ -195,25 +191,14 @@
     def spread(re, im, local_rows, cols):
         for comp, v in enumerate((butterfly8(re), butterfly8(im))):
             for t in range(8):
-                put_parts(comp * 8 + t, local_rows, cols, v[t])
+                big[comp * 8 + t, local_rows, cols] = v[t]
 
     def gather_big(local_rows, cols):
         re = butterfly8([big[t, local_rows, cols] for t in range(8)])
         im = butterfly8([big[8 + t, local_rows, cols] for t in range(8)])
         return re, im
 
-    def inverse_chunk(par, i):
-        for g in range(CHUNK // 16):
-            rows = pl.ds(pl.multiple_of(i * CHUNK + g * 16, 16), 16)
-            for ct in range(2):
-                for j in range(4):
-                    v = load_state(par, rows, cols_of(ct), j)
-                    for t, x in zip((j, 8 + j, 4 + j, 12 + j), v):
-                        put_parts(t, pl.ds(g * 16, 16), cols_of(ct), x)
-        right_multiply(big_write)
-
     def middle(layer, par, forward):
-        h = had[...]
         slot = lax.rem(layer, 2)
 
         def block(j, total, half):
@@ -221,7 +206,9 @@
             bits = half + j // 2 + lax.rem(j, 2)
             for comp in range(2):
                 src = keep[comp, j] if half == 0 else other[par, comp, j]
-                wide[comp] = dot3((h, h, h), split3(src))
+                flip[half * 2 + comp] = src.T
+            multiply([pair(flip.at[half * 2 + comp, pl.ds(r * STRIP, STRIP), :], wide.at[half * 2 + comp, pl.ds(r * STRIP, STRIP), :])
+                      for r in range(256 // STRIP) for comp in range(2)])
             for g in range(16):
                 rows = pl.ds(g * 16, 16)
                 for ct in range(2):
@@ -231,7 +218,7 @@
 
                     def pick(m):
                         return jnp.concatenate([diag[layer, m, bits + q0], diag[layer, m, bits + q1]], axis=0)
-                    re, im = wide[0, rows, cols], wide[1, rows, cols]
+                    re, im = wide[half * 2, rows, cols], wide[half * 2 + 1, rows, cols]
                     dc, ds = pick(0), pick(1)
                     if forward:
                         re, im = re * dc + im * ds, im * dc - re * ds
@@ -241,10 +228,12 @@
                         term = re * hat[slot, 1, n, rows, cols] - im * hat[slot, 0, n, rows, cols]
                         total = total + fold(term * pick(2))
                         re, im = re * dc - im * ds, im * dc + re * ds
-                    wide[0, rows, cols] = re
-                    wide[1, rows, cols] = im
+                    wide[half * 2, rows, cols] = re
+                    wide[half * 2 + 1, rows, cols] = im
+            multiply([pair(wide.at[half * 2 + comp, pl.ds(r * STRIP, STRIP), :], flip.at[half * 2 + comp, pl.ds(r * STRIP, STRIP), :])
+                      for r in range(256 // STRIP) for comp in range(2)])
             for comp in range(2):
-                value = dot3((h, h, h), split3(wide[comp]))
+                value = flip[half * 2 + comp].T
                 if half == 0:
                     keep[comp, j] = value
                 else:
@@ -258,16 +247,16 @@
     def tables():
         pop = popcount_tile((8, 128))
         for layer in range(LAYERS):
-            half_angle = jnp.full((8, 128), 0.5, F32) * beta[my_set, layer]
+            half_angle = jnp.full((8, 128), 0.25 / math.pi, F32) * beta[my_set, layer]
 
             def entry(q):
                 weight = (LOCAL_QUBITS - 2 * q).astype(F32) - 2.0 * pop
-                sin_d, cos_d = sincos(half_angle * weight)
+                sin_d, cos_d = sincos_turns(half_angle * weight)
                 diag[layer, 0, q] = cos_d * (2.0 ** -LOCAL_QUBITS)
                 diag[layer, 1, q] = sin_d * (2.0 ** -LOCAL_QUBITS)
                 diag[layer, 2, q] = weight
             loop(10, entry)
-            sin_h, cos_h = sincos(jnp.concatenate([half_angle, half_angle], axis=0))
+            sin_h, cos_h = sincos_turns(jnp.concatenate([half_angle, half_angle], axis=0))
             rot[layer + 1, 0] = cos_h
             rot[layer + 1, 1] = sin_h
         rot[0, 0] = jnp.ones((16, 128), F32)
@@ -286,11 +275,13 @@
         loop(16, init)
 
     def fill(layer, which, half, j):
+        turns = gamma[my_set, layer] * (0.5 / math.pi)
+
         def rows_body(r):
             start = pl.multiple_of(r * 32, 32)
             for ct in range(2):
                 cost_rows = pl.ds(pl.multiple_of(ct * 256 + start, 32), 32)
-                sin_p, cos_p = sincos(gamma[my_set, layer] * cc[which, j, cost_rows, :])
+                sin_p, cos_p = sincos_turns(turns * cc[which, j, cost_rows, :])
                 tab[layer, 0, half * 4 + j, pl.ds(start, 32), cols_of(ct)] = cos_p
                 tab[layer, 1, half * 4 + j, pl.ds(start, 32), cols_of(ct)] = sin_p
         loop(8, rows_body)
@@ -325,7 +316,7 @@
                         c, s = tab[layer, 0, n, rows, cols], tab[layer, 1, n, rows, cols]
                         re[n], im[n] = pr * c + pi * s, pi * c - pr * s
                 spread(re, im, local_rows, cols)
-            right_multiply(state_write(par, i))
+            to_state(par, i)
         loop(NUM_CHUNKS, alpha)
 
         @pl.when((layer >= 2))
@@ -338,7 +329,7 @@
             stash_out(layer).start()
 
         def gamma_sweep(i):
-            inverse_chunk(par, i)
+            from_state(par, i)
             for local_rows, rows, cols, _c in groups(i):
                 re, im = gather_big(local_rows, cols)
                 for j in range(4):
@@ -386,7 +377,7 @@
                 re = [v[j][0] for j in range(4)] + [v[j][2] for j in range(4)]
                 im = [v[j][1] for j in range(4)] + [v[j][3] for j in range(4)]
                 spread(re, im, local_rows, cols)
-            right_multiply(state_write(par, i))
+            to_state(par, i)
         loop(NUM_CHUNKS, alpha)
 
         @pl.when(layer < 3)
@@ -400,7 +391,7 @@
             stash_in(layer - 2).start()
 
         def gamma_sweep(i):
-            inverse_chunk(par, i)
+            from_state(par, i)
             g_sum = jnp.zeros((8, 128), F32)
             b_sum = jnp.zeros((8, 128), F32)
             cos_b, sin_b = rot[layer, 0], rot[layer, 1]
@@ -436,7 +427,7 @@
 
     def result_copy(a, b):
         return pltpu.make_async_remote_copy(
-            src_ref=mine, dst_ref=res.at[qx], send_sem=r_send.at[a * 4 + b], recv_sem=r_recv.at[qx],
+            src_ref=mine.at[0:NUM_ACC], dst_ref=res.at[qx], send_sem=r_send.at[a * 4 + b], recv_sem=r_recv.at[qx],
             device_id=(inst, a, b), device_id_type=MESH)
 
     def others(fn):
@@ -454,15 +445,15 @@
         loop(NUM_CHUNKS, final)
         send(0, NUM_CHUNKS - 1)
         loop(LAYERS, backward_layer)
-        mine[...] = jnp.sum(acc[...], axis=1)
-        res[qx] = mine[...]
+        mine[0:NUM_ACC] = jnp.sum(acc[...], axis=1)
+        res[qx] = mine[0:NUM_ACC]
         others(lambda copy: copy.start())
 
     for slot in range(4):
         @pl.when(jnp.logical_not(active & (qx == slot)))
         def _():
             pltpu.make_async_remote_copy(
-                src_ref=mine, dst_ref=res.at[slot], send_sem=r_send.at[0], recv_sem=r_recv.at[slot],
+                src_ref=mine.at[0:NUM_ACC], dst_ref=res.at[slot], send_sem=r_send.at[0], recv_sem=r_recv.at[slot],
                 device_id=partner, device_id_type=MESH).wait_recv()
 
     for s in range(2):
@@ -506,13 +497,13 @@
                 vmem((LAYERS, 2, 8) + tile, F32),
                 vmem((LAYERS, 2, 8) + tile, F32),
                 vmem((2, 2, 8) + tile, F32),
-                vmem((LAYERS, 3, 10, 8, 128), F32),
+                vmem((LAYERS, 3, 12, 8, 128), F32),
                 vmem((LAYERS + 1, 2, 16, 128), F32),
                 vmem((NUM_ACC, 8, 128), F32),
-                vmem((3, 16, CHUNK, 256), BF16),
-                vmem((2,) + tile, F32),
+                vmem((4,) + tile, F32),
+                vmem((4,) + tile, F32),
                 vmem((16, CHUNK, 256), F32),
-                vmem((NUM_ACC, 128), F32),
+                vmem((2 * NUM_ACC, 128), F32),
                 vmem((4, NUM_ACC, 128), F32),
                 dma((2,)), dma((2, 4)), dma((4,)), dma((4,)), dma((2, NUM_CHUNKS)), dma((2, NUM_CHUNKS)),
                 dma((2,)), dma((2,)), dma((16,)), dma((4,)), pltpu.SemaphoreType.REGULAR((NUM_CHUNKS,)),

time: 195 us -> 176 us (0.903)
  Pallas kernels: 191 us -> 171 us
    pallas_call x1, Pallas kernels: 191 us -> 171 us  [device_fn(): pl.pallas_call(kernel, out_shape=(jax.ShapeDtypeStruct((2, NUM_ACC, 128),...]
where the time goes in v2:
time: 176 us; the launch traced here: 175 us
  Pallas kernels  171 us (97%)
  local copies, waits for them, and re-layouts  2.67 us (2%)
    pallas_call x1, Pallas kernels, device_fn(): pl.pallas_call(kernel, out_shape=(jax.ShapeDtypeStruct((2, NUM_ACC, 128),...  171 us

profile of v2, /device:TPU:0, one launch (start us, length us, event | category | flops | bytes accessed | tf_op | source)
XLA Modules:
  0.0 175.5 jit_solution(1850746248766970096)
XLA Ops:
  0.6 0.9 subtract_convert_fusion.had
  1.5 171.3 %shard_map.50 = (f32[2,16,128]{2,1,0:T(8,128)}, f32[3,2,8,256,256]{4,3,2,1,0:T(8,128)}) custom-call(f32[512,128]{1,0:T(8,128)} %bitcast.1, f32[2,5]{1,0:T(2,128)} %gamma.1, f32[2,5]{1,0:T(2,128)} %beta.1, bf16[256,256]{1,0:T(8,128)(2,1)} %subtract_convert_fusion.had), custom_call_target="tpu_custom_call" | custom-call | tf_op jit(solution)/shard_map/pallas_call | solution.py:487
  172.8 1.3 slice_reduce_fusion.1
  174.1 1.4 slice_reduce_fusion

commit v3 on v2

--- a/solution.py
+++ b/solution.py
@@ -90,7 +90,7 @@
 
 
 def kernel(cost, gamma, beta, had, out, stash, keep, other, cc, tab, saved, hat, diag, rot, acc,
-           wide, flip, big, mine, res, c_send, c_recv, f_send, f_recv, x_send, x_recv, h_out, h_in, r_send, r_recv, credit):
+           wide, flip, big, mine, res, c_send, c_recv, f_send, f_recv, x_send, x_recv, h_out, h_in, r_send, r_recv, relay_send, relay_recv, credit):
     inst = lax.axis_index('inst')
     qy = lax.axis_index('qy')
     qx = lax.axis_index('qx')
@@ -100,24 +100,63 @@
     partner = (inst, qy, qx + 1 - 2 * core)
     kind = lax.rem(qy // 2 + qy, 2)
 
-    def cost_copy(s):
+    def view(s):
+        return (qy, qx, qx // 2) if s == 0 else (3 - qy, qx, 1 - qx // 2)
+
+    def home_copy(s, src, origin_y, origin_x, send_sem):
         home_y, home_x = HOMES[s]
+        slot = lax.rem(origin_y // 2 + origin_y, 2)
         return pltpu.make_async_remote_copy(
-            src_ref=cost, dst_ref=cc.at[kind, qx], send_sem=c_send.at[s], recv_sem=c_recv.at[kind, qx],
-            device_id=(inst, home_y, home_x + qy // 2), device_id_type=MESH)
+            src_ref=src, dst_ref=cc.at[slot, origin_x], send_sem=send_sem, recv_sem=c_recv.at[slot, origin_x],
+            device_id=(inst, home_y, home_x + origin_y // 2), device_id_type=MESH)
+
+    def relay_copy(s, to_y, to_x, r):
+        return pltpu.make_async_remote_copy(
+            src_ref=cost, dst_ref=cc.at[2, r], send_sem=c_send.at[s], recv_sem=relay_recv.at[r],
+            device_id=(inst, to_y, to_x), device_id_type=MESH)
 
     def is_self(s):
         home_y, home_x = HOMES[s]
         return (qy == home_y) & (qx == home_x + qy // 2)
 
+    def routes(s):
+        y, _x, side = view(s)
+        near_y = 1 if s == 0 else 2
+        corner_y = 0 if s == 0 else 3
+        corner_x = qx - 2 if s == 0 else qx + 2
+        direct = jnp.logical_not(is_self(s)) & ((side == 0) | (y == 1))
+        return [(direct, home_copy(s, cost, qy, qx, c_send.at[s])),
+                ((side == 1) & (y == 0), relay_copy(s, corner_y, corner_x, 0)),
+                ((side == 1) & (y == 2), relay_copy(s, near_y, qx, 0)),
+                ((side == 1) & (y == 3), relay_copy(s, near_y, qx, 1))]
+
+    def relays(s):
+        y, _x, side = view(s)
+        corner_y = 0 if s == 0 else 3
+        corner_x = qx + 2 if s == 0 else qx - 2
+        far = (2, 3) if s == 0 else (1, 0)
+        out = [((side == 0) & (y == 0), 0, home_copy(s, cc.at[2, 0], corner_y, corner_x, relay_send.at[0]))]
+        for r in range(2):
+            out.append(((side == 1) & (y == 1), r, home_copy(s, cc.at[2, r], far[r], qx, relay_send.at[r])))
+        return out
+
+    def relay_wait(r):
+        pltpu.make_async_copy(cost, cc.at[2, r], relay_recv.at[r]).wait()
+
     for s in range(2):
         @pl.when(is_self(s))
         def _():
             pltpu.make_async_copy(cost, cc.at[kind, qx], c_recv.at[kind, qx]).start()
 
-        @pl.when(jnp.logical_not(is_self(s)))
-        def _():
-            cost_copy(s).start()
+        for condition, copy in routes(s):
+            pl.when(condition)(copy.start)
+
+    for s in range(2):
+        for condition, r, copy in relays(s):
+            @pl.when(condition)
+            def _():
+                relay_wait(r)
+                copy.start()
 
     def cost_arrived(which, j):
         pltpu.make_async_copy(cost, cc.at[which, j], c_recv.at[which, j]).wait()
@@ -286,14 +325,22 @@
                 tab[layer, 1, half * 4 + j, pl.ds(start, 32), cols_of(ct)] = sin_p
         loop(8, rows_body)
 
-    def arrive(j):
-        cost_arrived(1, j)
-        forward_copy(j).start()
-        loop(3, lambda n: fill(2 * n, 1, 1, j))
-        cost_arrived(0, j)
-        loop(LAYERS, lambda n: fill(n, 0, 0, j))
-        forward_copy(j).wait()
-        loop(2, lambda n: fill(2 * n + 1, 2, 1, j))
+    def arrive():
+        def own(j):
+            cost_arrived(1, j)
+            forward_copy(j).start()
+            loop(3, lambda n: fill(2 * n, 1, 1, j))
+
+        def passed(j):
+            forward_copy(j).wait()
+            loop(2, lambda n: fill(2 * n + 1, 2, 1, j))
+
+        def kept(j):
+            cost_arrived(0, j)
+            loop(LAYERS, lambda n: fill(n, 0, 0, j))
+        loop(4, own)
+        loop(4, passed)
+        loop(4, kept)
 
     def forward_layer(layer):
         par = lax.rem(layer, 2)
@@ -335,11 +382,8 @@
                 for j in range(4):
                     store_state(par, rows, cols, j, (re[j], im[j], re[4 + j], im[4 + j]))
 
-            @pl.when(i > 0)
-            def _():
-                send(1 - par, i - 1, layer == 0)
+            send(1 - par, i, layer == 0)
         loop(NUM_CHUNKS, gamma_sweep)
-        send(1 - par, NUM_CHUNKS - 1, layer == 0)
 
     def final(i):
         exchange(1, i).wait()
@@ -358,9 +402,7 @@
         acc[0] = acc[0] + energy
         acc[2 * LAYERS] = acc[2 * LAYERS] + grad
 
-        @pl.when(i > 0)
-        def _():
-            send(0, i - 1)
+        send(0, i)
 
     def backward_layer(step):
         layer = LAYERS - 1 - step
@@ -416,14 +458,10 @@
             def _():
                 acc[LAYERS + layer] = acc[LAYERS + layer] + b_sum
 
-            @pl.when((i > 0) & (layer > 0))
+            @pl.when(layer > 0)
             def _():
-                send(1 - par, i - 1)
+                send(1 - par, i)
         loop(NUM_CHUNKS, gamma_sweep)
-
-        @pl.when(layer > 0)
-        def _():
-            send(1 - par, NUM_CHUNKS - 1)
 
     def result_copy(a, b):
         return pltpu.make_async_remote_copy(
@@ -440,10 +478,9 @@
     @pl.when(active)
     def _():
         tables()
-        loop(4, arrive)
+        arrive()
         loop(LAYERS, forward_layer)
         loop(NUM_CHUNKS, final)
-        send(0, NUM_CHUNKS - 1)
         loop(LAYERS, backward_layer)
         mine[0:NUM_ACC] = jnp.sum(acc[...], axis=1)
         res[qx] = mine[0:NUM_ACC]
@@ -463,7 +500,10 @@
     for s in range(2):
         @pl.when(jnp.logical_not(is_self(s)))
         def _():
-            cost_copy(s).wait_send()
+            home_copy(s, cost, qy, qx, c_send.at[s]).wait_send()
+
+        for condition, r, copy in relays(s):
+            pl.when(condition)(copy.wait_send)
 
     @pl.when(active)
     def _():
@@ -471,12 +511,10 @@
 
 
 def hadamard():
-    index = jnp.arange(256, dtype=jnp.int32)
+    index = np.arange(256)
     both = index[:, None] & index[None, :]
-    parity = jnp.zeros((256, 256), jnp.int32)
-    for b in range(8):
-        parity = parity ^ ((both >> b) & 1)
-    return (1 - 2 * parity).astype(BF16)
+    parity = sum((both >> b) & 1 for b in range(8)) & 1
+    return jnp.asarray(1.0 - 2.0 * parity, BF16)
 
 
 def solution(mesh):
@@ -506,7 +544,7 @@
                 vmem((2 * NUM_ACC, 128), F32),
                 vmem((4, NUM_ACC, 128), F32),
                 dma((2,)), dma((2, 4)), dma((4,)), dma((4,)), dma((2, NUM_CHUNKS)), dma((2, NUM_CHUNKS)),
-                dma((2,)), dma((2,)), dma((16,)), dma((4,)), pltpu.SemaphoreType.REGULAR((NUM_CHUNKS,)),
+                dma((2,)), dma((2,)), dma((16,)), dma((4,)), dma((2,)), dma((2,)), pltpu.SemaphoreType.REGULAR((NUM_CHUNKS,)),
             ],
             compiler_params=pltpu.CompilerParams(has_side_effects=True, vmem_limit_bytes=67043328),
         )(cost.reshape(512, 128), gamma, beta, hadamard())

time: 176 us -> 169 us (0.960)
  Pallas kernels: 171 us -> 165 us
    pallas_call x1, Pallas kernels: 171 us -> 165 us  [device_fn(): pl.pallas_call(kernel, out_shape=(jax.ShapeDtypeStruct((2, NUM_ACC, 128),...]
where the time goes in v3:
time: 169 us; the launch traced here: 168 us
  Pallas kernels  165 us (98%)
  local copies, waits for them, and re-layouts  2.67 us (2%)
    pallas_call x1, Pallas kernels, device_fn(): pl.pallas_call(kernel, out_shape=(jax.ShapeDtypeStruct((2, NUM_ACC, 128),...  165 us

profile of v3, /device:TPU:0, one launch (start us, length us, event | category | flops | bytes accessed | tf_op | source)
XLA Modules:
  0.0 168.3 jit_solution(2943344373331250733)
XLA Ops:
  0.6 165.0 %shard_map.59 = (f32[2,16,128]{2,1,0:T(8,128)}, f32[3,2,8,256,256]{4,3,2,1,0:T(8,128)}) custom-call(f32[512,128]{1,0:T(8,128)} %bitcast.1, f32[2,5]{1,0:T(2,128)} %gamma.1, f32[2,5]{1,0:T(2,128)} %beta.1, bf16[256,256]{1,0:T(8,128)(2,1)} %constant.2.clone.had), custom_call_target="tpu_custom_call" | custom-call | tf_op jit(solution)/shard_map/pallas_call | solution.py:525
  165.6 1.3 slice_reduce_fusion.1
  166.9 1.4 slice_reduce_fusion

commit v4 on v3

--- a/solution.py
+++ b/solution.py
@@ -18,6 +18,7 @@
 SIN = (3.14159265353629, -5.16771276462444, 2.550163318944362, -0.5992521977957433, 0.08205040168394097, -0.00702838621010907)
 COS = (0.9999999997799045, -4.9348021370788056, 4.058709159555753, -1.3352120030448535, 0.23493731379172217, -0.024396324310603436)
 MESH = pl.DeviceIdType.MESH
+PARTS = tuple(pl.ds(n * 64, 64) for n in range(8))
 HOMES = ((1, 0), (2, 2))
 
 
@@ -103,17 +104,20 @@
     def view(s):
         return (qy, qx, qx // 2) if s == 0 else (3 - qy, qx, 1 - qx // 2)
 
-    def home_copy(s, src, origin_y, origin_x, send_sem):
+    def home_copy(s, src, origin_y, origin_x, send_sem, part=None):
         home_y, home_x = HOMES[s]
         slot = lax.rem(origin_y // 2 + origin_y, 2)
+        dst = cc.at[slot, origin_x]
+        if part is not None:
+            src, dst = src.at[part], dst.at[part]
         return pltpu.make_async_remote_copy(
-            src_ref=src, dst_ref=cc.at[slot, origin_x], send_sem=send_sem, recv_sem=c_recv.at[slot, origin_x],
+            src_ref=src, dst_ref=dst, send_sem=send_sem, recv_sem=c_recv.at[slot, origin_x],
             device_id=(inst, home_y, home_x + origin_y // 2), device_id_type=MESH)
 
-    def relay_copy(s, to_y, to_x, r):
-        return pltpu.make_async_remote_copy(
-            src_ref=cost, dst_ref=cc.at[2, r], send_sem=c_send.at[s], recv_sem=relay_recv.at[r],
-            device_id=(inst, to_y, to_x), device_id_type=MESH)
+    def relay_copies(s, to_y, to_x, r):
+        return [pltpu.make_async_remote_copy(
+            src_ref=cost.at[part], dst_ref=cc.at[2, r].at[part], send_sem=c_send.at[s], recv_sem=relay_recv.at[r, n],
+            device_id=(inst, to_y, to_x), device_id_type=MESH) for n, part in enumerate(PARTS)]
 
     def is_self(s):
         home_y, home_x = HOMES[s]
@@ -125,38 +129,38 @@
         corner_y = 0 if s == 0 else 3
         corner_x = qx - 2 if s == 0 else qx + 2
         direct = jnp.logical_not(is_self(s)) & ((side == 0) | (y == 1))
-        return [(direct, home_copy(s, cost, qy, qx, c_send.at[s])),
-                ((side == 1) & (y == 0), relay_copy(s, corner_y, corner_x, 0)),
-                ((side == 1) & (y == 2), relay_copy(s, near_y, qx, 0)),
-                ((side == 1) & (y == 3), relay_copy(s, near_y, qx, 1))]
+        return [(direct, [home_copy(s, cost, qy, qx, c_send.at[s])]),
+                ((side == 1) & (y == 0), relay_copies(s, corner_y, corner_x, 0)),
+                ((side == 1) & (y == 2), relay_copies(s, near_y, qx, 0)),
+                ((side == 1) & (y == 3), relay_copies(s, near_y, qx, 1))]
 
     def relays(s):
         y, _x, side = view(s)
         corner_y = 0 if s == 0 else 3
         corner_x = qx + 2 if s == 0 else qx - 2
         far = (2, 3) if s == 0 else (1, 0)
-        out = [((side == 0) & (y == 0), 0, home_copy(s, cc.at[2, 0], corner_y, corner_x, relay_send.at[0]))]
-        for r in range(2):
-            out.append(((side == 1) & (y == 1), r, home_copy(s, cc.at[2, r], far[r], qx, relay_send.at[r])))
-        return out
-
-    def relay_wait(r):
-        pltpu.make_async_copy(cost, cc.at[2, r], relay_recv.at[r]).wait()
+        return [((side == 0) & (y == 0), [(0, corner_y, corner_x)]),
+                ((side == 1) & (y == 1), [(r, far[r], qx) for r in range(2)])]
 
     for s in range(2):
         @pl.when(is_self(s))
         def _():
             pltpu.make_async_copy(cost, cc.at[kind, qx], c_recv.at[kind, qx]).start()
 
-        for condition, copy in routes(s):
-            pl.when(condition)(copy.start)
+        for condition, copies in routes(s):
+            @pl.when(condition)
+            def _():
+                for copy in copies:
+                    copy.start()
 
     for s in range(2):
-        for condition, r, copy in relays(s):
+        for condition, blocks in relays(s):
             @pl.when(condition)
             def _():
-                relay_wait(r)
-                copy.start()
+                for n, part in enumerate(PARTS):
+                    for r, origin_y, origin_x in blocks:
+                        pltpu.make_async_copy(cost.at[part], cc.at[2, r].at[part], relay_recv.at[r, n]).wait()
+                        home_copy(s, cc.at[2, r], origin_y, origin_x, relay_send.at[r], part).start()
 
     def cost_arrived(which, j):
         pltpu.make_async_copy(cost, cc.at[which, j], c_recv.at[which, j]).wait()
@@ -338,9 +342,15 @@
         def kept(j):
             cost_arrived(0, j)
             loop(LAYERS, lambda n: fill(n, 0, 0, j))
-        loop(4, own)
-        loop(4, passed)
-        loop(4, kept)
+        def near_then_far(step):
+            near = lax.rem(step + my_set, 2) * 2
+            loop(2, lambda n: own(near + n))
+
+            @pl.when(step == 1)
+            def _():
+                loop(4, passed)
+            loop(2, lambda n: kept(near + n))
+        loop(2, near_then_far)
 
     def forward_layer(layer):
         par = lax.rem(layer, 2)
@@ -502,8 +512,11 @@
         def _():
             home_copy(s, cost, qy, qx, c_send.at[s]).wait_send()
 
-        for condition, r, copy in relays(s):
-            pl.when(condition)(copy.wait_send)
+        for condition, blocks in relays(s):
+            @pl.when(condition)
+            def _():
+                for r, origin_y, origin_x in blocks:
+                    home_copy(s, cc.at[2, r], origin_y, origin_x, relay_send.at[r]).wait_send()
 
     @pl.when(active)
     def _():
@@ -544,7 +557,7 @@
                 vmem((2 * NUM_ACC, 128), F32),
                 vmem((4, NUM_ACC, 128), F32),
                 dma((2,)), dma((2, 4)), dma((4,)), dma((4,)), dma((2, NUM_CHUNKS)), dma((2, NUM_CHUNKS)),
-                dma((2,)), dma((2,)), dma((16,)), dma((4,)), dma((2,)), dma((2,)), pltpu.SemaphoreType.REGULAR((NUM_CHUNKS,)),
+                dma((2,)), dma((2,)), dma((16,)), dma((4,)), dma((2,)), dma((2, len(PARTS))), pltpu.SemaphoreType.REGULAR((NUM_CHUNKS,)),
             ],
             compiler_params=pltpu.CompilerParams(has_side_effects=True, vmem_limit_bytes=67043328),
         )(cost.reshape(512, 128), gamma, beta, hadamard())

time: 169 us -> 163 us (0.964)
  Pallas kernels: 165 us -> 160 us
    pallas_call x1, Pallas kernels: 165 us -> 160 us  [device_fn(): pl.pallas_call(kernel, out_shape=(jax.ShapeDtypeStruct((2, NUM_ACC, 128),...]
where the time goes in v4:
time: 163 us
  Pallas kernels  160 us (98%)
  local copies, waits for them, and re-layouts  2.67 us (2%)
    pallas_call x1, Pallas kernels, device_fn(): pl.pallas_call(kernel, out_shape=(jax.ShapeDtypeStruct((2, NUM_ACC, 128),...  160 us

profile of v4, /device:TPU:0, one launch (start us, length us, event | category | flops | bytes accessed | tf_op | source)
XLA Modules:
  0.0 162.9 jit_solution(3283829089223534455)
XLA Ops:
  0.6 159.6 %shard_map.59 = (f32[2,16,128]{2,1,0:T(8,128)}, f32[3,2,8,256,256]{4,3,2,1,0:T(8,128)}) custom-call(f32[512,128]{1,0:T(8,128)} %bitcast.1, f32[2,5]{1,0:T(2,128)} %gamma.1, f32[2,5]{1,0:T(2,128)} %beta.1, bf16[256,256]{1,0:T(8,128)(2,1)} %constant.2.clone.had), custom_call_target="tpu_custom_call" | custom-call | tf_op jit(solution)/shard_map/pallas_call | solution.py:538
  160.2 1.3 slice_reduce_fusion.1
  161.5 1.4 slice_reduce_fusion

commit v5 on v4

--- a/solution.py
+++ b/solution.py
@@ -101,6 +101,14 @@
     partner = (inst, qy, qx + 1 - 2 * core)
     kind = lax.rem(qy // 2 + qy, 2)
 
+    barrier = pltpu.get_barrier_semaphore()
+    for a in range(4):
+        for b in range(4):
+            @pl.when((qy != a) | (qx != b))
+            def _():
+                pl.semaphore_signal(barrier, inc=1, device_id=(inst, a, b), device_id_type=MESH)
+    pl.semaphore_wait(barrier, 15)
+
     def view(s):
         return (qy, qx, qx // 2) if s == 0 else (3 - qy, qx, 1 - qx // 2)
 
@@ -244,14 +252,16 @@
     def middle(layer, par, forward):
         slot = lax.rem(layer, 2)
 
-        def block(j, total, half):
-            n = half * 4 + j
-            bits = half + j // 2 + lax.rem(j, 2)
+        def first(j, half):
             for comp in range(2):
                 src = keep[comp, j] if half == 0 else other[par, comp, j]
                 flip[half * 2 + comp] = src.T
             multiply([pair(flip.at[half * 2 + comp, pl.ds(r * STRIP, STRIP), :], wide.at[half * 2 + comp, pl.ds(r * STRIP, STRIP), :])
-                      for r in range(256 // STRIP) for comp in range(2)])
+                      for comp in range(2) for r in range(256 // STRIP)])
+
+        def second(j, total, half):
+            n = half * 4 + j
+            bits = half + j // 2 + lax.rem(j, 2)
             for g in range(16):
                 rows = pl.ds(g * 16, 16)
                 for ct in range(2):
@@ -274,7 +284,7 @@
                     wide[half * 2, rows, cols] = re
                     wide[half * 2 + 1, rows, cols] = im
             multiply([pair(wide.at[half * 2 + comp, pl.ds(r * STRIP, STRIP), :], flip.at[half * 2 + comp, pl.ds(r * STRIP, STRIP), :])
-                      for r in range(256 // STRIP) for comp in range(2)])
+                      for comp in range(2) for r in range(256 // STRIP)])
             for comp in range(2):
                 value = flip[half * 2 + comp].T
                 if half == 0:
@@ -284,7 +294,9 @@
             return total
 
         def body(j, total):
-            return block(j, block(j, total, 0), 1)
+            first(j, 0)
+            first(j, 1)
+            return second(j, second(j, total, 0), 1)
         return lax.fori_loop(0, 4, body, jnp.zeros((8, 128), F32))
 
     def tables():
@@ -559,7 +571,7 @@
                 dma((2,)), dma((2, 4)), dma((4,)), dma((4,)), dma((2, NUM_CHUNKS)), dma((2, NUM_CHUNKS)),
                 dma((2,)), dma((2,)), dma((16,)), dma((4,)), dma((2,)), dma((2, len(PARTS))), pltpu.SemaphoreType.REGULAR((NUM_CHUNKS,)),
             ],
-            compiler_params=pltpu.CompilerParams(has_side_effects=True, vmem_limit_bytes=67043328),
+            compiler_params=pltpu.CompilerParams(collective_id=0, has_side_effects=True, vmem_limit_bytes=67043328),
         )(cost.reshape(512, 128), gamma, beta, hadamard())
         return out[:, 0, 0], out[:, 1:1 + 2 * LAYERS, 0]
 

time: 163 us -> 161 us (0.988)
  Pallas kernels: 160 us -> 158 us
    pallas_call x1, Pallas kernels: 160 us -> 158 us  [device_fn(): pl.pallas_call(kernel, out_shape=(jax.ShapeDtypeStruct((2, NUM_ACC, 128),...]
where the time goes in v5:
time: 161 us
  Pallas kernels  158 us (98%)
  local copies, waits for them, and re-layouts  2.67 us (2%)
    pallas_call x1, Pallas kernels, device_fn(): pl.pallas_call(kernel, out_shape=(jax.ShapeDtypeStruct((2, NUM_ACC, 128),...  158 us

profile of v5, /device:TPU:0, one launch (start us, length us, event | category | flops | bytes accessed | tf_op | source)
XLA Modules:
  0.0 161.0 jit_solution(15453073235975244329)
XLA Ops:
  0.6 157.7 %shard_map.59 = (f32[2,16,128]{2,1,0:T(8,128)}, f32[3,2,8,256,256]{4,3,2,1,0:T(8,128)}) custom-call(f32[512,128]{1,0:T(8,128)} %bitcast.1, f32[2,5]{1,0:T(2,128)} %gamma.1, f32[2,5]{1,0:T(2,128)} %beta.1, bf16[256,256]{1,0:T(8,128)(2,1)} %constant.2.clone.had), custom_call_target="tpu_custom_call" | custom-call | tf_op jit(solution)/shard_map/pallas_call | solution.py:550
  158.4 1.3 slice_reduce_fusion.1
  159.7 1.4 slice_reduce_fusion

commit v6 on v5

--- a/solution.py
+++ b/solution.py
@@ -18,7 +18,7 @@
 SIN = (3.14159265353629, -5.16771276462444, 2.550163318944362, -0.5992521977957433, 0.08205040168394097, -0.00702838621010907)
 COS = (0.9999999997799045, -4.9348021370788056, 4.058709159555753, -1.3352120030448535, 0.23493731379172217, -0.024396324310603436)
 MESH = pl.DeviceIdType.MESH
-PARTS = tuple(pl.ds(n * 64, 64) for n in range(8))
+PARTS = tuple(pl.ds(n * 128, 128) for n in range(4))
 HOMES = ((1, 0), (2, 2))
 
 
@@ -357,10 +357,7 @@
         def near_then_far(step):
             near = lax.rem(step + my_set, 2) * 2
             loop(2, lambda n: own(near + n))
-
-            @pl.when(step == 1)
-            def _():
-                loop(4, passed)
+            loop(2, lambda n: passed(near + n))
             loop(2, lambda n: kept(near + n))
         loop(2, near_then_far)
 

time: 161 us -> 160 us (level)
  Pallas kernels: 158 us -> 156 us
    pallas_call x1, Pallas kernels: 158 us -> 156 us  [device_fn(): pl.pallas_call(kernel, out_shape=(jax.ShapeDtypeStruct((2, NUM_ACC, 128),...]
where the time goes in v6:
time: 160 us; the launch traced here: 159 us
  Pallas kernels  156 us (98%)
  local copies, waits for them, and re-layouts  2.67 us (2%)
    pallas_call x1, Pallas kernels, device_fn(): pl.pallas_call(kernel, out_shape=(jax.ShapeDtypeStruct((2, NUM_ACC, 128),...  156 us

profile of v6, /device:TPU:0, one launch (start us, length us, event | category | flops | bytes accessed | tf_op | source)
XLA Modules:
  0.0 159.3 jit_solution(2183757845033766433)
XLA Ops:
  0.6 156.0 %shard_map.59 = (f32[2,16,128]{2,1,0:T(8,128)}, f32[3,2,8,256,256]{4,3,2,1,0:T(8,128)}) custom-call(f32[512,128]{1,0:T(8,128)} %bitcast.1, f32[2,5]{1,0:T(2,128)} %gamma.1, f32[2,5]{1,0:T(2,128)} %beta.1, bf16[256,256]{1,0:T(8,128)(2,1)} %constant.2.clone.had), custom_call_target="tpu_custom_call" | custom-call | tf_op jit(solution)/shard_map/pallas_call | solution.py:547
  156.7 1.3 slice_reduce_fusion.1
  158.0 1.4 slice_reduce_fusion
